TPU v7x, 768 devices: a whole 4x8x12 slice. The times are simulated.
768 devices in a mesh: gx: 128 (over z_hi, y, x, core), gz: 6 (over z_lo).
Axes of the slice: x: 4, y: 8, z: 12 (z_hi: 2, z_lo: 6; z = z_hi * 6 + z_lo), core: 2. Of those that a mesh axis runs over, the one named last changes fastest.
Arguments:
- state: float32 [5, 1024, 16, 768], P(None, 'gx', None, 'gz'), may hold values from -1 to 8.5, as said below
- register: float32 [5, 1024, 16, 768], P(None, 'gx', None, 'gz'), may hold values from -2.4 to 2.4
- top_ghost: float32 [5, 1024, 3, 768], P(None, 'gx', None, 'gz'), may hold values from -1 to 8.5, as said below
- flags: int32 [1024, 16, 6], P('gx', None, 'gz'), may hold values 0 or 1
Outputs:
- new_state: float32 [5, 1024, 16, 768], P(None, 'gx', None, 'gz')
- new_register: float32 [5, 1024, 16, 768], P(None, 'gx', None, 'gz')
Inputs may be any that keep to these rules, and one draw needn't show every extreme that they name: `state`: conserved variables of an ideal gas with ratio of heats 1.4, density 0.5 to 2 and pressure 0.3 to 1.5 in every cell. `top_ghost`: conserved variables of an ideal gas with ratio of heats 1.4, density 0.5 to 2 and pressure 0.3 to 1.5 in every cell.
All inputs are finite; a program needn't handle non-finite values. No bound on the sum of `flags` on one device may be relied on, other than what follows from the above.
Results may differ from a plain program's by a relative error of at most 0.0003.
Values sent between devices are 32-bit elements; how exact they have to be, the bound alone decides.
No kernel may reach another device: no remote copies, remote signals or barrier semaphores. Data moves between devices by JAX's collectives and lax.ppermute only.
A program may use at most 32 MiB of HBM per device.

v0:
```python
import functools

import jax
import jax.numpy as jnp
from jax import lax
from jax.sharding import Mesh
from jax.sharding import PartitionSpec as P

ZBLOCK = 128
GX_GZ = ("gx_0", "gx_1", "gx_2", "gx_3", "gz")
GX = ("gx_0", "gx_1", "gx_2", "gx_3")


GAMMA = 1.4
EPS_WENO = 1e-06
LAMBDA_X = 0.1
LAMBDA_Y = 0.15
LAMBDA_Z = 0.1
REGISTER_DECAY = -5.0 / 9.0
UPDATE_WEIGHT = 15.0 / 16.0


def by_axis(value, axes):
    return functools.reduce(lax.pmax, axes, value)


def with_halo(value, sides, width):
    edges = {}
    for axis, dim in sides:
        size, length = (lax.axis_size(axis), value.shape[dim])
        up = [(i, (i + 1) % size) for i in range(size)]
        last = lax.slice_in_dim(value, length - width, length, axis=dim)
        first = lax.slice_in_dim(value, 0, width, axis=dim)
        edges[dim] = (
            lax.ppermute(last, axis, up),
            lax.ppermute(first, axis, [(b, a) for a, b in up]),
        )
    done = []
    for _, dim in sides:
        low, high = edges[dim]
        around = [(width, width) if d in done else (0, 0) for d in range(value.ndim)]
        value = jnp.concatenate([jnp.pad(low, around), value, jnp.pad(high, around)], axis=dim)
        done.append(dim)
    return value


def primitives(cons):
    density = cons[0]
    inverse = 1.0 / density
    vel_x = cons[1] * inverse
    vel_y = cons[2] * inverse
    vel_z = cons[3] * inverse
    pressure = (GAMMA - 1.0) * (
        cons[4] - 0.5 * (cons[1] * vel_x + cons[2] * vel_y + cons[3] * vel_z)
    )
    return (density, vel_x, vel_y, vel_z, pressure)


def global_speeds(prims):
    density, vel_x, vel_y, vel_z, pressure = prims
    sound = jnp.sqrt(GAMMA * pressure / density)
    local = jnp.stack(
        [
            jnp.max(jnp.abs(vel_x) + sound),
            jnp.max(jnp.abs(vel_y) + sound),
            jnp.max(jnp.abs(vel_z) + sound),
        ]
    )
    return by_axis(local, GX_GZ)


def physical_flux(cons, prims, var):
    pressure = prims[4]
    velocity = prims[var]
    rows = [
        cons[0] * velocity,
        cons[1] * velocity,
        cons[2] * velocity,
        cons[3] * velocity,
        (cons[4] + pressure) * velocity,
    ]
    rows[var] = rows[var] + pressure
    return jnp.stack(rows)


def weno_face(vals):
    first, second, third, fourth, fifth = vals
    cand_a = (2.0 * first - 7.0 * second + 11.0 * third) / 6.0
    cand_b = (-second + 5.0 * third + 2.0 * fourth) / 6.0
    cand_c = (2.0 * third + 5.0 * fourth - fifth) / 6.0
    smooth_a = (
        13.0 / 12.0 * (first - 2.0 * second + third) ** 2
        + 0.25 * (first - 4.0 * second + 3.0 * third) ** 2
    )
    smooth_b = 13.0 / 12.0 * (second - 2.0 * third + fourth) ** 2 + 0.25 * (second - fourth) ** 2
    smooth_c = (
        13.0 / 12.0 * (third - 2.0 * fourth + fifth) ** 2
        + 0.25 * (3.0 * third - 4.0 * fourth + fifth) ** 2
    )
    weight_a = 0.1 / (EPS_WENO + smooth_a) ** 2
    weight_b = 0.6 / (EPS_WENO + smooth_b) ** 2
    weight_c = 0.3 / (EPS_WENO + smooth_c) ** 2
    return (weight_a * cand_a + weight_b * cand_b + weight_c * cand_c) / (
        weight_a + weight_b + weight_c
    )


def divergence(padded, prims, alpha, var, axis_pos, count, cell_flag):
    flux = physical_flux(padded, prims, var)
    plus = 0.5 * (flux + alpha * padded)
    minus = 0.5 * (flux - alpha * padded)

    def window(arr, offset):
        return lax.slice_in_dim(arr, offset, offset + count + 1, axis=axis_pos)

    central = (
        37.0 * (window(flux, 2) + window(flux, 3))
        - 8.0 * (window(flux, 1) + window(flux, 4))
        + (window(flux, 0) + window(flux, 5))
    ) / 60.0
    upwind = weno_face(
        [window(plus, 0), window(plus, 1), window(plus, 2), window(plus, 3), window(plus, 4)]
    )
    upwind = upwind + weno_face(
        [window(minus, 5), window(minus, 4), window(minus, 3), window(minus, 2), window(minus, 1)]
    )

    def jump(face):
        return lax.slice_in_dim(face, 1, count + 1, axis=axis_pos) - lax.slice_in_dim(
            face, 0, count, axis=axis_pos
        )

    return jnp.where(cell_flag[None], jump(upwind), jump(central))


def wall_pad(inner, top_ghost):
    mirror = jnp.array([1.0, 1.0, -1.0, 1.0, 1.0], dtype=jnp.float32).reshape(5, 1, 1, 1)
    lower = jnp.flip(inner[:, :, :3], axis=2) * mirror
    return jnp.concatenate([lower, inner, top_ghost], axis=2)


def expand_flags(flags):
    shape = flags.shape
    wide = jnp.broadcast_to(flags[:, :, :, None], (shape[0], shape[1], shape[2], ZBLOCK))
    return wide.reshape(shape[0], shape[1], shape[2] * ZBLOCK) > 0


def shards(state, register, top_ghost, flags):
    cell_flag = expand_flags(flags)
    both_pad = with_halo(state, ((GX, 1), ("gz", 3)), 3)
    x_pad = both_pad[:, :, :, 3:-3]
    z_pad = both_pad[:, 3:-3]
    y_pad = wall_pad(state, top_ghost)
    x_prims = primitives(x_pad)
    alpha = global_speeds(primitives(state))
    div_x = divergence(x_pad, x_prims, alpha[0], 1, 1, state.shape[1], cell_flag)
    div_y = divergence(y_pad, primitives(y_pad), alpha[1], 2, 2, state.shape[2], cell_flag)
    div_z = divergence(z_pad, primitives(z_pad), alpha[2], 3, 3, state.shape[3], cell_flag)
    change = -(LAMBDA_X * div_x + LAMBDA_Y * div_y + LAMBDA_Z * div_z)
    new_register = REGISTER_DECAY * register + change
    new_state = state + UPDATE_WEIGHT * new_register
    return (new_state, new_register)


def solution(mesh):
    finer = Mesh(
        mesh.devices.reshape(2, 8, 4, 2, mesh.shape["gz"]), ("gx_0", "gx_1", "gx_2", "gx_3", "gz")
    )
    placed = (
        P(None, GX, None, "gz"),
        P(None, GX, None, "gz"),
        P(None, GX, None, "gz"),
        P(GX, None, "gz"),
    )
    return jax.shard_map(
        shards,
        mesh=finer,
        in_specs=placed,
        out_specs=(P(None, GX, None, "gz"), P(None, GX, None, "gz")),
        check_vma=False,
    )
```

profile of v0, /device:TPU:10, one launch (start us, length us, event | category | flops | bytes accessed | tf_op | source)
XLA Modules:
  0.0 113.4 jit_solution(13385413818724207952)
XLA Ops:
  0.6 1.1 %copy.19 = f32[5,8,16,128]{3,1,2,0:T(8,128)S(1)} copy(f32[5,8,16,128]{3,2,1,0:T(8,128)} %param.5) | data formatting | bytes 655360 | tf_op args[0]
  1.8 0.1 fusion.51
  1.9 1.9 %collective-permute-start = (f32[5,3,16,128]{3,1,2,0:T(4,128)S(1)}, f32[5,3,16,128]{3,1,2,0:T(4,128)S(1)}, u32[]{:S(2)}, u32[]{:S(2)}) collective-permute-start(f32[5,3,16,128]{3,1,2,0:T(4,128)S(1)} %get-tuple-element.27), channel_id=1, source_target_pairs={{0,6},{6,12},{12,18},{18,24},{24,30},{30,36},{36,42},{42,48},{48,5... | collective-permute-start | bytes 368648 | tf_op jit(solution)/shard_map/ppermute | solution.py:35
  3.8 0.7 add_reduce_fusion.2
  4.5 1.9 %pad_maximum_fusion.2 = f32[3]{0:T(128)S(1)} fusion(f32[1]{0:T(128)} %bitcast.9, f32[1]{0:T(128)} %bitcast.8, f32[1]{0:T(128)} %bitcast.7), kind=kLoop, calls=%fused_computation.122 | loop fusion | flops 6 | bytes 24 | tf_op jit(solution)/shard_map/stack | solution.py:62
  6.4 3.6 %collective-permute-start.1 = (f32[5,3,16,128]{3,1,2,0:T(4,128)S(1)}, f32[5,3,16,128]{3,1,2,0:T(4,128)S(1)}, u32[]{:S(2)}, u32[]{:S(2)}) collective-permute-start(f32[5,3,16,128]{3,1,2,0:T(4,128)S(1)} %get-tuple-element.28), channel_id=1, source_target_pairs={{6,0},{12,6},{18,12},{24,18},{30,24},{36,30},{42,36},{48,42},{54,4... | collective-permute-start | bytes 368648 | tf_op jit(solution)/shard_map/ppermute | solution.py:36
  10.0 16.1 %pmax.35 = f32[3]{0:T(128)S(1)} all-reduce(f32[3]{0:T(128)S(1)} %pad_maximum_fusion.2), channel_id=1, replica_groups=mesh['gx_0'=2,'gx_1'=8,'gx_2'=4,'gx_3'=2,'gz'=6] {'gx_0'}, use_global_device_ids=true, to_apply=%region_3.4 | all-reduce | flops 3 | bytes 24 | tf_op jit(solution)/shard_map/pmax | solution.py:24
  26.2 0.2 fusion.52
  26.3 16.2 %pmax.36 = f32[3]{0:T(128)S(1)} all-reduce(f32[3]{0:T(128)S(1)} %pmax.35), channel_id=1, replica_groups=mesh['gx_0'=2,'gx_1'=8,'gx_2'=4,'gx_3'=2,'gz'=6] {'gx_1'}, use_global_device_ids=true, to_apply=%region_4.5 | all-reduce | flops 3 | bytes 24 | tf_op jit(solution)/shard_map/pmax | solution.py:24
  42.5 3.4 %collective-permute-start.2 = (f32[5,8,16,3]{3,1,2,0:T(8,128)S(1)}, f32[5,8,16,3]{3,1,2,0:T(8,128)S(1)}, u32[]{:S(2)}, u32[]{:S(2)}) collective-permute-start(f32[5,8,16,3]{3,1,2,0:T(8,128)S(1)} %get-tuple-element.29), channel_id=1, source_target_pairs={{0,1},{1,2},{2,3},{3,4},{4,5},{5,0},{6,7},{7,8},{8,9},{9,10},{10,1... | collective-permute-start | bytes 23048 | tf_op jit(solution)/shard_map/ppermute | solution.py:35
  45.9 19.8 %pmax.37 = f32[3]{0:T(128)S(1)} all-reduce(f32[3]{0:T(128)S(1)} %pmax.36), channel_id=1, replica_groups=mesh['gx_0'=2,'gx_1'=8,'gx_2'=4,'gx_3'=2,'gz'=6] {'gx_2'}, use_global_device_ids=true, to_apply=%region_5.6 | all-reduce | flops 3 | bytes 24 | tf_op jit(solution)/shard_map/pmax | solution.py:24
  65.7 8.7 %collective-permute-start.3 = (f32[5,8,16,3]{3,1,2,0:T(8,128)S(1)}, f32[5,8,16,3]{3,1,2,0:T(8,128)S(1)}, u32[]{:S(2)}, u32[]{:S(2)}) collective-permute-start(f32[5,8,16,3]{3,1,2,0:T(8,128)S(1)} %get-tuple-element.30), channel_id=1, source_target_pairs={{1,0},{2,1},{3,2},{4,3},{5,4},{0,5},{7,6},{8,7},{9,8},{10,9},{11,1... | collective-permute-start | bytes 23048 | tf_op jit(solution)/shard_map/ppermute | solution.py:36
  74.5 2.5 %pmax.38 = f32[3]{0:T(128)S(1)} all-reduce(f32[3]{0:T(128)S(1)} %pmax.37), channel_id=1, replica_groups=mesh['gx_0'=2,'gx_1'=8,'gx_2'=4,'gx_3'=2,'gz'=6] {'gx_3'}, use_global_device_ids=true, to_apply=%region_6.7 | all-reduce | flops 3 | bytes 24 | tf_op jit(solution)/shard_map/pmax | solution.py:24
  77.0 19.8 %pmax.39 = f32[3]{0:T(128)S(1)} all-reduce(f32[3]{0:T(128)S(1)} %pmax.38), channel_id=1, replica_groups=mesh['gx_0'=2,'gx_1'=8,'gx_2'=4,'gx_3'=2,'gz'=6] {'gz'}, use_global_device_ids=true, to_apply=%region_7.8 | all-reduce | flops 3 | bytes 24 | tf_op jit(solution)/shard_map/pmax | solution.py:24
  96.8 0.6 fusion.53
  97.4 0.1 reverse_multiply_fusion
  97.6 0.6 add_multiply_fusion.2
  98.3 1.6 %fusion.11 = (f32[5,8,17,128]{3,1,2,0:T(8,128)S(1)}, f32[5,8,17,128]{3,1,2,0:T(8,128)S(1)}) fusion(f32[5,8,22,128]{3,1,2,0:T(8,128)S(1)} %multiply_dynamic-update-slice_fusion.8, f32[5,8,22,128]{3,1,2,0:T(8,128)S(1)} %get-tuple-element.26, f32[5,8,22,128]{3,1,2,0:T(8,128)S(1)} %get-tuple-element.25), kind=kLoop, calls=%fused_computation.33 | loop fusion | flops 11924480 | bytes 6266880 | tf_op jit(solution)/shard_map/div | solution.py:116
  99.9 0.1 copy.11
  100.1 0.9 select_maximum_fusion
  101.1 0.1 add_dynamic-update-slice_fusion
  101.3 0.9 fusion.1
  102.2 0.8 add_multiply_fusion
  103.0 0.1 pad_maximum_fusion
  103.2 0.1 add_dynamic-update-slice_fusion.1
  103.3 0.4 fusion.6
  103.7 3.3 %divide_add_fusion = f32[5,8,16,129]{3,1,2,0:T(8,128)S(1)} fusion(f32[5,8,16,134]{3,1,2,0:T(8,128)S(1)} %get-tuple-element.22, f32[5,8,16,134]{3,1,2,0:T(8,128)S(1)} %get-tuple-element.21), kind=kLoop, calls=%fused_computation.22 | loop fusion | flops 10650240 | bytes 3632640 | tf_op jit(solution)/shard_map/add | solution.py:124
  107.0 0.9 add_multiply_fusion.1
  107.9 3.3 %divide_add_fusion.1 = f32[5,9,16,128]{3,1,2,0:T(8,128)S(1)} fusion(f32[5,14,16,128]{3,1,2,0:T(8,128)S(1)} %get-tuple-element.24, f32[5,14,16,128]{3,1,2,0:T(8,128)S(1)} %get-tuple-element.23), kind=kLoop, calls=%fused_computation.25 | loop fusion | flops 11888640 | bytes 4055040 | tf_op jit(solution)/shard_map/add | solution.py:124
  111.2 0.6 multiply_add_fusion
  111.9 0.8 copy.20
  112.6 0.8 copy.21
  (30 shorter events, 0.4 us)
Async XLA Ops:
  0.6 3.2 %copy-start = (f32[5,8,16,128]{3,2,1,0:T(8,128)S(1)}, f32[5,8,16,128]{3,2,1,0:T(8,128)}, u32[]{:S(2)}) copy-start(f32[5,8,16,128]{3,2,1,0:T(8,128)} %param.5) | copy-start | bytes 983044
  1.8 95.6 %copy-start.4 = (f32[5]{0:T(128)S(1)}, f32[5]{0:T(128)}, u32[]{:S(2)}) copy-start(f32[5]{0:T(128)} %constant.53.clone) | copy-start | bytes 64
  1.8 95.6 %copy-start.2 = (f32[5,8,3,128]{3,1,2,0:T(8,128)S(1)}, f32[5,8,3,128]{3,1,2,0:T(8,128)}, u32[]{:S(2)}) copy-start(f32[5,8,3,128]{3,1,2,0:T(8,128)} %param.7) | copy-start | bytes 184324
  1.9 98.2 %collective-permute-start = (f32[5,3,16,128]{3,1,2,0:T(4,128)S(1)}, f32[5,3,16,128]{3,1,2,0:T(4,128)S(1)}, u32[]{:S(2)}, u32[]{:S(2)}) collective-permute-start(f32[5,3,16,128]{3,1,2,0:T(4,128)S(1)} %get-tuple-element.27), channel_id=1, source_target_pairs={{0,6},{6,12},{12,18},{18,24},{24,30},{30,36},{36,42},{42,48},{48,5... | collective-permute-start | bytes 368648 | tf_op jit(solution)/shard_map/ppermute | solution.py:35
  6.4 93.7 %collective-permute-start.1 = (f32[5,3,16,128]{3,1,2,0:T(4,128)S(1)}, f32[5,3,16,128]{3,1,2,0:T(4,128)S(1)}, u32[]{:S(2)}, u32[]{:S(2)}) collective-permute-start(f32[5,3,16,128]{3,1,2,0:T(4,128)S(1)} %get-tuple-element.28), channel_id=1, source_target_pairs={{6,0},{12,6},{18,12},{24,18},{30,24},{36,30},{42,36},{48,42},{54,4... | collective-permute-start | bytes 368648 | tf_op jit(solution)/shard_map/ppermute | solution.py:36
  42.5 57.5 %collective-permute-start.2 = (f32[5,8,16,3]{3,1,2,0:T(8,128)S(1)}, f32[5,8,16,3]{3,1,2,0:T(8,128)S(1)}, u32[]{:S(2)}, u32[]{:S(2)}) collective-permute-start(f32[5,8,16,3]{3,1,2,0:T(8,128)S(1)} %get-tuple-element.29), channel_id=1, source_target_pairs={{0,1},{1,2},{2,3},{3,4},{4,5},{5,0},{6,7},{7,8},{8,9},{9,10},{10,1... | collective-permute-start | bytes 23048 | tf_op jit(solution)/shard_map/ppermute | solution.py:35
  65.7 34.3 %collective-permute-start.3 = (f32[5,8,16,3]{3,1,2,0:T(8,128)S(1)}, f32[5,8,16,3]{3,1,2,0:T(8,128)S(1)}, u32[]{:S(2)}, u32[]{:S(2)}) collective-permute-start(f32[5,8,16,3]{3,1,2,0:T(8,128)S(1)} %get-tuple-element.30), channel_id=1, source_target_pairs={{1,0},{2,1},{3,2},{4,3},{5,4},{0,5},{7,6},{8,7},{9,8},{10,9},{11,1... | collective-permute-start | bytes 23048 | tf_op jit(solution)/shard_map/ppermute | solution.py:36
  98.3 1.7 %copy-start.3 = (s32[8,16,1]{1,2,0:T(1,128)S(1)}, s32[8,16,1]{1,2,0:T(1,128)}, u32[]{:S(2)}) copy-start(s32[8,16,1]{1,2,0:T(1,128)} %param.8) | copy-start | bytes 1540
  107.9 3.3 %copy-start.1 = (f32[5,8,16,128]{3,2,1,0:T(8,128)S(1)}, f32[5,8,16,128]{3,2,1,0:T(8,128)}, u32[]{:S(2)}) copy-start(f32[5,8,16,128]{3,2,1,0:T(8,128)} %param.6) | copy-start | bytes 983044
where the time goes:
time: 114 us; the launch traced here: 113 us
  blocking collectives  74.5 us (65%)
  starting transfers between devices  17.6 us (15%)
  other arithmetic  16.8 us (15%)
  local copies, waits for them, and re-layouts  3.63 us (3%)
    pmax x5, blocking collectives, by_axis(): return functools.reduce(lax.pmax, axes, value)  74.5 us
    ppermute x2, starting transfers between devices, with_halo(): lax.ppermute(first, axis, [(b, a) for a, b in up])  12.3 us
    add x2, other arithmetic, divergence(): upwind + weno_face([window(minus, 5), window(minus, 4), window(minus, 3),...  6.6 us
    ppermute x2, starting transfers between devices, with_halo(): lax.ppermute(last, axis, up)  5.29 us
    div x3, other arithmetic, divergence(): (37.0 * (window(flux, 2) + window(flux, 3)) - 8.0 * (window(flux, 1) + wi...  2.93 us
    unnamed x13, local copies, waits for them, and re-layouts  2.74 us
    mul x3, other arithmetic, divergence(): plus = 0.5 * (flux + alpha * padded)  2.34 us
  transfers between devices with their start and end apart: 4, of which 0 were waited for; matrix products, arithmetic and copies ran while one was open for 5% of the time, Pallas kernels for 0%

commit v1 on v0

--- a/solution.py
+++ b/solution.py
@@ -20,8 +20,14 @@
 UPDATE_WEIGHT = 15.0 / 16.0
 
 
+def max_over(value, axes):
+    size = functools.reduce(lambda a, b: a * b, [lax.axis_size(a) for a in axes])
+    sent = jnp.broadcast_to(value[None], (size, value.shape[0]))
+    return jnp.max(lax.all_to_all(sent, axes, 0, 0, tiled=True), axis=0)
+
+
 def by_axis(value, axes):
-    return functools.reduce(lax.pmax, axes, value)
+    return max_over(max_over(value, ("gx_1", "gx_2", "gx_3")), ("gx_0", "gz"))
 
 
 def with_halo(value, sides, width):

time: 114 us -> 84 us (0.74)
  the two profiles are of different devices: /device:TPU:10 before, /device:TPU:64 now
where the time goes in v1:
time: 84 us; the launch traced here: 83.6 us
  starting transfers between devices  51.5 us (61%)
  other arithmetic  17.8 us (21%)
  waiting for transfers between devices  8.5 us (10%)
  local copies, waits for them, and re-layouts  4.83 us (6%)
  between operations  0.97 us (1%)
    all_to_all x2, starting transfers between devices, max_over(): return jnp.max(lax.all_to_all(sent, axes, 0, 0, tiled=True), axis=0)  25.1 us
    ppermute x2, starting transfers between devices, with_halo(): lax.ppermute(first, axis, [(b, a) for a, b in up])  21.6 us
    all_to_all x2, waiting for transfers between devices, max_over(): return jnp.max(lax.all_to_all(sent, axes, 0, 0, tiled=True), axis=0)  8.49 us
    add x2, other arithmetic, divergence(): upwind + weno_face([window(minus, 5), window(minus, 4), window(minus, 3),...  6.6 us
    ppermute x2, starting transfers between devices, with_halo(): lax.ppermute(last, axis, up)  4.74 us
    div x3, other arithmetic, divergence(): (37.0 * (window(flux, 2) + window(flux, 3)) - 8.0 * (window(flux, 1) + wi...  2.93 us
    unnamed x13, local copies, waits for them, and re-layouts  2.7 us
    mul x3, other arithmetic, divergence(): plus = 0.5 * (flux + alpha * padded)  2.34 us
  transfers between devices with their start and end apart: 6, of which 1 were waited for; matrix products, arithmetic and copies ran while one was open for 6% of the time, Pallas kernels for 0%

profile of v1, /device:TPU:64, one launch (start us, length us, event | category | flops | bytes accessed | tf_op | source)
XLA Modules:
  0.0 83.6 jit_solution(10234566518788781566)
XLA Ops:
  0.6 1.7 %add_reduce_fusion.2 = (f32[]{:T(128)}, f32[]{:T(128)}, f32[]{:T(128)}) fusion(f32[5,8,16,128]{3,2,1,0:T(8,128)} %param.5), kind=kLoop, calls=%fused_computation.119 | loop fusion | flops 360445 | bytes 327692 | tf_op jit(solution)/shard_map/reduce_max | solution.py:70
  2.3 1.9 %pad_maximum_fusion.2 = f32[3]{0:T(128)S(1)} fusion(f32[1]{0:T(128)} %bitcast.9, f32[1]{0:T(128)} %bitcast.8, f32[1]{0:T(128)} %bitcast.7), kind=kLoop, calls=%fused_computation.122 | loop fusion | flops 6 | bytes 24 | tf_op jit(solution)/shard_map/stack | solution.py:68
  4.2 0.6 broadcast_in_dim.19
  4.8 10.6 %all-to-all-start = ((f32[64,1,3]{2,1,0:T(1,128)}), f32[64,1,3]{2,1,0:T(1,128)S(1)}, u32[]{:S(2)}, u32[]{:S(2)}) async-start(f32[64,1,3]{2,1,0:T(1,128)} %broadcast_in_dim.19), calls=%async_computation | async-start | bytes 65536 | tf_op jit(solution)/shard_map/all_to_all | solution.py:26
  15.4 1.1 %copy.31 = f32[5,8,16,128]{3,1,2,0:T(8,128)S(1)} copy(f32[5,8,16,128]{3,2,1,0:T(8,128)} %param.5) | data formatting | bytes 655360 | tf_op args[0]
  16.6 2.0 %collective-permute-start = (f32[5,3,16,128]{3,1,2,0:T(4,128)S(1)}, f32[5,3,16,128]{3,1,2,0:T(4,128)S(1)}, u32[]{:S(2)}, u32[]{:S(2)}) collective-permute-start(f32[5,3,16,128]{3,1,2,0:T(4,128)S(1)} %get-tuple-element.27), channel_id=1, source_target_pairs={{0,6},{6,12},{12,18},{18,24},{24,30},{30,36},{36,42},{42,48},{48,5... | collective-permute-start | bytes 368648 | tf_op jit(solution)/shard_map/ppermute | solution.py:41
  18.6 18.6 %collective-permute-start.1 = (f32[5,3,16,128]{3,1,2,0:T(4,128)S(1)}, f32[5,3,16,128]{3,1,2,0:T(4,128)S(1)}, u32[]{:S(2)}, u32[]{:S(2)}) collective-permute-start(f32[5,3,16,128]{3,1,2,0:T(4,128)S(1)} %get-tuple-element.28), channel_id=1, source_target_pairs={{6,0},{12,6},{18,12},{24,18},{30,24},{36,30},{42,36},{48,42},{54,4... | collective-permute-start | bytes 368648 | tf_op jit(solution)/shard_map/ppermute | solution.py:42
  37.1 0.2 fusion.52
  37.3 2.8 %collective-permute-start.2 = (f32[5,8,16,3]{3,1,2,0:T(8,128)S(1)}, f32[5,8,16,3]{3,1,2,0:T(8,128)S(1)}, u32[]{:S(2)}, u32[]{:S(2)}) collective-permute-start(f32[5,8,16,3]{3,1,2,0:T(8,128)S(1)} %get-tuple-element.29), channel_id=1, source_target_pairs={{0,1},{1,2},{2,3},{3,4},{4,5},{5,0},{6,7},{7,8},{8,9},{9,10},{10,1... | collective-permute-start | bytes 23048 | tf_op jit(solution)/shard_map/ppermute | solution.py:41
  40.1 3.1 %collective-permute-start.3 = (f32[5,8,16,3]{3,1,2,0:T(8,128)S(1)}, f32[5,8,16,3]{3,1,2,0:T(8,128)S(1)}, u32[]{:S(2)}, u32[]{:S(2)}) collective-permute-start(f32[5,8,16,3]{3,1,2,0:T(8,128)S(1)} %get-tuple-element.30), channel_id=1, source_target_pairs={{1,0},{2,1},{3,2},{4,3},{5,4},{0,5},{7,6},{8,7},{9,8},{10,9},{11,1... | collective-permute-start | bytes 23048 | tf_op jit(solution)/shard_map/ppermute | solution.py:42
  43.2 0.1 reverse_multiply_fusion
  43.5 0.1 reduce_max.48
  43.6 0.6 broadcast_in_dim.20
  44.2 14.5 %all-to-all-start.1 = ((f32[12,1,3]{2,1,0:T(1,128)}), f32[12,1,3]{2,1,0:T(1,128)S(1)}, u32[]{:S(2)}, u32[]{:S(2)}) async-start(f32[12,1,3]{2,1,0:T(1,128)} %broadcast_in_dim.20), calls=%async_computation.1 | async-start | bytes 12288 | tf_op jit(solution)/shard_map/all_to_all | solution.py:26
  58.7 0.1 copy.21
  58.8 8.5 %all-to-all-done.1 = f32[12,1,3]{2,1,0:T(1,128)S(1)} async-done(((f32[12,1,3]{2,1,0:T(1,128)}), f32[12,1,3]{2,1,0:T(1,128)S(1)}, u32[]{:S(2)}, u32[]{:S(2)}) %all-to-all-start.1) | async-done | bytes 176 | tf_op jit(solution)/shard_map/all_to_all | solution.py:26
  67.3 0.6 fusion.53
  67.9 0.7 add_multiply_fusion.2
  68.6 1.6 %fusion.11 = (f32[5,8,17,128]{3,1,2,0:T(8,128)S(1)}, f32[5,8,17,128]{3,1,2,0:T(8,128)S(1)}) fusion(f32[5,8,22,128]{3,1,2,0:T(8,128)S(1)} %multiply_dynamic-update-slice_fusion.8, f32[5,8,22,128]{3,1,2,0:T(8,128)S(1)} %get-tuple-element.26, f32[5,8,22,128]{3,1,2,0:T(8,128)S(1)} %get-tuple-element.25), kind=kLoop, calls=%fused_computation.33 | loop fusion | flops 11924480 | bytes 6266880 | tf_op jit(solution)/shard_map/div | solution.py:122
  70.3 0.9 %select_maximum_fusion = f32[5,14,16,134]{3,1,2,0:T(8,128)S(1)} fusion(f32[5,8,16,3]{3,1,2,0:T(8,128)S(1)} %collective-permute-done.3, f32[5,8,16,3]{3,1,2,0:T(8,128)S(1)} %collective-permute-done.2, f32[5,3,16,128]{3,1,2,0:T(4,128)S(1)} %collective-permute-done.1, f32[5,8,16,128]{3,1,2,0:T(8,128)S(1)} %copy.31, f32[5,3,16,128]{3,1,2,0:T(4,128)S(1)} %collective-permute-done), kind=kLoop, calls=%fused_computation | loop fusion | flops 1200640 | bytes 1189120 | tf_op jit(solution)/shard_map/concatenate | solution.py:48
  71.4 0.1 add_dynamic-update-slice_fusion
  71.5 0.9 %fusion.1 = f32[5,8,16,129]{3,1,2,0:T(8,128)S(1)} fusion(f32[5,8,16,134]{3,1,2,0:T(8,128)S(1)} %multiply_dynamic-update-slice_fusion), kind=kLoop, calls=%fused_computation.6 | loop fusion | flops 660480 | bytes 2311680 | tf_op jit(solution)/shard_map/div | solution.py:122
  72.4 0.7 add_multiply_fusion
  73.2 0.1 pad_maximum_fusion
  73.4 0.1 add_dynamic-update-slice_fusion.1
  73.5 0.4 fusion.6
  73.9 3.3 %divide_add_fusion = f32[5,8,16,129]{3,1,2,0:T(8,128)S(1)} fusion(f32[5,8,16,134]{3,1,2,0:T(8,128)S(1)} %get-tuple-element.22, f32[5,8,16,134]{3,1,2,0:T(8,128)S(1)} %get-tuple-element.21), kind=kLoop, calls=%fused_computation.22 | loop fusion | flops 10650240 | bytes 3632640 | tf_op jit(solution)/shard_map/add | solution.py:130
  77.2 0.9 %add_multiply_fusion.1 = (f32[5,14,16,128]{3,1,2,0:T(8,128)S(1)}, f32[5,14,16,128]{3,1,2,0:T(8,128)S(1)}) fusion(f32[5,14,16,128]{3,1,2,0:T(8,128)S(1)} %multiply_dynamic-update-slice_fusion.4, f32[]{:T(128)} %bitcast.10, f32[5,3,16,128]{3,1,2,0:T(4,128)S(1)} %collective-permute-done.1, f32[5,8,16,128]{3,1,2,0:T(8,128)S(1)} %copy.31, ...), kind=kLoop, calls=%fused_computation.27 | loop fusion | flops 1003520 | bytes 2293764 | tf_op jit(solution)/shard_map/mul | solution.py:116
  78.1 3.3 %divide_add_fusion.1 = f32[5,9,16,128]{3,1,2,0:T(8,128)S(1)} fusion(f32[5,14,16,128]{3,1,2,0:T(8,128)S(1)} %get-tuple-element.24, f32[5,14,16,128]{3,1,2,0:T(8,128)S(1)} %get-tuple-element.23), kind=kLoop, calls=%fused_computation.25 | loop fusion | flops 11888640 | bytes 4055040 | tf_op jit(solution)/shard_map/add | solution.py:130
  81.4 0.6 multiply_add_fusion
  82.0 0.8 copy.32
  82.8 0.8 copy.33
  (33 shorter events, 0.5 us)
Async XLA Ops:
  4.8 38.6 %all-to-all-start = ((f32[64,1,3]{2,1,0:T(1,128)}), f32[64,1,3]{2,1,0:T(1,128)S(1)}, u32[]{:S(2)}, u32[]{:S(2)}) async-start(f32[64,1,3]{2,1,0:T(1,128)} %broadcast_in_dim.19), calls=%async_computation | async-start | bytes 65536 | tf_op jit(solution)/shard_map/all_to_all | solution.py:26
  15.4 27.8 %copy-start.4 = (f32[5]{0:T(128)S(1)}, f32[5]{0:T(128)}, u32[]{:S(2)}) copy-start(f32[5]{0:T(128)} %constant.53.clone) | copy-start | bytes 64
  15.4 27.8 %copy-start.2 = (f32[5,8,3,128]{3,1,2,0:T(8,128)S(1)}, f32[5,8,3,128]{3,1,2,0:T(8,128)}, u32[]{:S(2)}) copy-start(f32[5,8,3,128]{3,1,2,0:T(8,128)} %param.7) | copy-start | bytes 184324
  16.6 53.7 %collective-permute-start = (f32[5,3,16,128]{3,1,2,0:T(4,128)S(1)}, f32[5,3,16,128]{3,1,2,0:T(4,128)S(1)}, u32[]{:S(2)}, u32[]{:S(2)}) collective-permute-start(f32[5,3,16,128]{3,1,2,0:T(4,128)S(1)} %get-tuple-element.27), channel_id=1, source_target_pairs={{0,6},{6,12},{12,18},{18,24},{24,30},{30,36},{36,42},{42,48},{48,5... | collective-permute-start | bytes 368648 | tf_op jit(solution)/shard_map/ppermute | solution.py:41
  18.6 51.7 %collective-permute-start.1 = (f32[5,3,16,128]{3,1,2,0:T(4,128)S(1)}, f32[5,3,16,128]{3,1,2,0:T(4,128)S(1)}, u32[]{:S(2)}, u32[]{:S(2)}) collective-permute-start(f32[5,3,16,128]{3,1,2,0:T(4,128)S(1)} %get-tuple-element.28), channel_id=1, source_target_pairs={{6,0},{12,6},{18,12},{24,18},{30,24},{36,30},{42,36},{48,42},{54,4... | collective-permute-start | bytes 368648 | tf_op jit(solution)/shard_map/ppermute | solution.py:42
  37.3 33.0 %collective-permute-start.2 = (f32[5,8,16,3]{3,1,2,0:T(8,128)S(1)}, f32[5,8,16,3]{3,1,2,0:T(8,128)S(1)}, u32[]{:S(2)}, u32[]{:S(2)}) collective-permute-start(f32[5,8,16,3]{3,1,2,0:T(8,128)S(1)} %get-tuple-element.29), channel_id=1, source_target_pairs={{0,1},{1,2},{2,3},{3,4},{4,5},{5,0},{6,7},{7,8},{8,9},{9,10},{10,1... | collective-permute-start | bytes 23048 | tf_op jit(solution)/shard_map/ppermute | solution.py:41
  40.1 30.2 %collective-permute-start.3 = (f32[5,8,16,3]{3,1,2,0:T(8,128)S(1)}, f32[5,8,16,3]{3,1,2,0:T(8,128)S(1)}, u32[]{:S(2)}, u32[]{:S(2)}) collective-permute-start(f32[5,8,16,3]{3,1,2,0:T(8,128)S(1)} %get-tuple-element.30), channel_id=1, source_target_pairs={{1,0},{2,1},{3,2},{4,3},{5,4},{0,5},{7,6},{8,7},{9,8},{10,9},{11,1... | collective-permute-start | bytes 23048 | tf_op jit(solution)/shard_map/ppermute | solution.py:42
  43.3 15.4 %copy-start.3 = (s32[8,16,1]{1,2,0:T(1,128)S(1)}, s32[8,16,1]{1,2,0:T(1,128)}, u32[]{:S(2)}) copy-start(s32[8,16,1]{1,2,0:T(1,128)} %param.8) | copy-start | bytes 1540
  44.2 23.1 %all-to-all-start.1 = ((f32[12,1,3]{2,1,0:T(1,128)}), f32[12,1,3]{2,1,0:T(1,128)S(1)}, u32[]{:S(2)}, u32[]{:S(2)}) async-start(f32[12,1,3]{2,1,0:T(1,128)} %broadcast_in_dim.20), calls=%async_computation.1 | async-start | bytes 12288 | tf_op jit(solution)/shard_map/all_to_all | solution.py:26
  78.1 3.4 %copy-start = (f32[5,8,16,128]{3,2,1,0:T(8,128)S(1)}, f32[5,8,16,128]{3,2,1,0:T(8,128)}, u32[]{:S(2)}) copy-start(f32[5,8,16,128]{3,2,1,0:T(8,128)} %param.5) | copy-start | bytes 983044
  78.1 3.4 %copy-start.1 = (f32[5,8,16,128]{3,2,1,0:T(8,128)S(1)}, f32[5,8,16,128]{3,2,1,0:T(8,128)}, u32[]{:S(2)}) copy-start(f32[5,8,16,128]{3,2,1,0:T(8,128)} %param.6) | copy-start | bytes 983044

commit v2 on v0

v2 whole, which is shorter than its diff:
```python
import jax
import jax.numpy as jnp
from jax import lax
from jax.experimental import pallas as pl
from jax.experimental.pallas import tpu as pltpu
from jax.sharding import Mesh
from jax.sharding import PartitionSpec as P

GX = ("gx_0", "gx_1", "gx_2", "gx_3")
PLANE = ("gx_1", "gx_2", "gx_3")
ZLINE = ("gx_0", "gz")

GAMMA = 1.4
EPS_WENO = 1e-06
LAMBDA = (0.1, 0.15, 0.1)
REGISTER_DECAY = -5.0 / 9.0
UPDATE_WEIGHT = 15.0 / 16.0

NV = 5
CX = 8
CY = 16
CZ = 128
ROWS = CX * CY
HALO = 3
SUB = 8
LONG = 16 + 2 * HALO
WIDE = CX + 2 * HALO


def primitives(cons):
    inverse = 1.0 / cons[0]
    vels = [cons[k] * inverse for k in (1, 2, 3)]
    kinetic = cons[1] * vels[0] + cons[2] * vels[1] + cons[3] * vels[2]
    pressure = (GAMMA - 1.0) * (cons[4] - 0.5 * kinetic)
    return inverse, vels, pressure


def speed_kernel(state_ref, out_ref):
    best = [None] * 3
    for block in range(ROWS // SUB):
        rows = slice(block * SUB, block * SUB + SUB)
        inverse, vels, pressure = primitives([state_ref[v, rows, :] for v in range(NV)])
        sound = jnp.sqrt(GAMMA * pressure * inverse)
        for k in range(3):
            speed = jnp.abs(vels[k]) + sound
            best[k] = speed if block == 0 else jnp.maximum(best[k], speed)
    lane = lax.broadcasted_iota(jnp.int32, (1, CZ), 1)
    packed = jnp.zeros((1, CZ), jnp.float32)
    for k in range(3):
        top = jnp.max(jnp.max(best[k], axis=0, keepdims=True), axis=1, keepdims=True)
        packed = jnp.where(lane == k, top, packed)
    for to in range(out_ref.shape[0]):
        out_ref[to] = packed


def relay_kernel(got_ref, out_ref):
    best = got_ref[0]
    for i in range(1, got_ref.shape[0]):
        best = jnp.maximum(best, got_ref[i])
    for to in range(out_ref.shape[0]):
        out_ref[to] = best


def edges_kernel(state_ref, turned_ref, first_ref, last_ref):
    for v in range(NV):
        turned = state_ref[v].T
        turned_ref[v] = turned
        first_ref[v] = turned[:HALO]
        last_ref[v] = turned[CZ - HALO :]


def split_flux(cons, var, alpha):
    _, vels, pressure = primitives(cons)
    velocity = vels[var - 1]
    plus, minus = [], []
    for v in range(NV):
        carried = cons[v] + pressure if v == 4 else cons[v]
        flux = carried * velocity
        if v == var:
            flux = flux + pressure
        moved = alpha * cons[v]
        plus.append(flux + moved)
        minus.append(flux - moved)
    return plus, minus


EPS_SCALED = 16.0 * EPS_WENO
CURVE = 13.0 / 3.0


def faces(plus, minus, count):
    total = [p + m for p, m in zip(plus, minus)]

    def slopes(vals):
        step = [b - a for a, b in zip(vals, vals[1:])]
        bend = [None] + [b - a for a, b in zip(step, step[1:])]
        base = [None] + [CURVE * (d * d) + EPS_SCALED for d in bend[1:]]
        return step, bend, base

    pe, pd, pk = slopes(plus)
    me, md, mk = slopes(minus)

    def blend(ta, ka, tb, kb, tc, kc, va, vb, vc):
        ba, bb, bc_ = ka + ta * ta, kb + tb * tb, kc + tc * tc
        x, y, z = bb * bc_, ba * bc_, ba * bb
        wa, wb, wc = x * x, 6.0 * (y * y), 3.0 * (z * z)
        return (wa * va + wb * vb + wc * vc) / (wa + wb + wc)

    ups, cens = [], []
    for j in range(count):
        bc, cd = pe[j + 1], pe[j + 2]
        ta = pd[j + 1] + (bc + bc)
        tb = bc + cd
        tc = pd[j + 3] - (cd + cd)
        up = blend(ta, pk[j + 1], tb, pk[j + 2], tc, pk[j + 3], (ta + ta) - bc, tb + cd, cd - tc)
        bc, cd = me[j + 3], me[j + 2]
        ta = md[j + 4] - (bc + bc)
        tb = bc + cd
        tc = md[j + 2] + (cd + cd)
        down = blend(ta, mk[j + 4], tb, mk[j + 3], tc, mk[j + 2], (ta + ta) + bc, -(tb + cd), -(cd + tc))
        ups.append(6.0 * (plus[j + 2] + minus[j + 3]) + (up + down))
        cens.append(
            37.0 * (total[j + 2] + total[j + 3])
            - 8.0 * (total[j + 1] + total[j + 4])
            + (total[j] + total[j + 5])
        )
    return ups, cens


def jumps(plus, minus, count, masks, scale):
    ups, cens = faces(plus, minus, count + 1)
    return [
        jnp.where(masks[i], (scale / 12.0) * (ups[i + 1] - ups[i]), (scale / 120.0) * (cens[i + 1] - cens[i]))
        for i in range(count)
    ]


def step_kernel(
    speed_ref, state_ref, turned_ref, xlo_ref, xhi_ref, xlo_seam_ref, xhi_seam_ref, zlo_ref, zhi_ref,
    top_ref, flag_ref, reg_ref,
    new_state_ref, new_reg_ref,
    xp, xm, yp, ym, zp, zm, line, mask, acc_y, acc_z,
):
    best = speed_ref[0]
    for i in range(1, speed_ref.shape[0]):
        best = jnp.maximum(best, speed_ref[i])
    lane = lax.broadcasted_iota(jnp.int32, (1, CZ), 1)
    alphas = [jnp.max(jnp.where(lane == k, best, 0.0), axis=1, keepdims=True) for k in range(3)]

    for block in range(ROWS // SUB):
        rows = slice(block * SUB, block * SUB + SUB)
        mask[rows, :] = jnp.broadcast_to(flag_ref[rows, :].astype(jnp.float32), (SUB, CZ))
    turned_mask = mask[...].T[:SUB]

    def x_plane(i, rest_ref, seam_ref, shift):
        for h in range(CY // SUB):
            rows = pl.ds(h * SUB, SUB)
            cons = [rest_ref[v, i, rows, :] + seam_ref[v, i, rows, :] for v in range(NV)]
            plus, minus = split_flux(cons, 1, alphas[0])
            for v in range(NV):
                xp[v, i + shift, rows, :] = plus[v]
                xm[v, i + shift, rows, :] = minus[v]

    for i in range(HALO):
        x_plane(i, xlo_ref, xlo_seam_ref, 0)
        x_plane(i, xhi_ref, xhi_seam_ref, HALO + CX)

    def x_body(i, carry):
        for h in range(CY // SUB):
            rows = pl.ds(pl.multiple_of(i * CY + h * SUB, SUB), SUB)
            plus, minus = split_flux([state_ref[v, rows, :] for v in range(NV)], 1, alphas[0])
            for v in range(NV):
                xp[v, i + HALO, pl.ds(h * SUB, SUB), :] = plus[v]
                xm[v, i + HALO, pl.ds(h * SUB, SUB), :] = minus[v]
        return carry

    lax.fori_loop(0, CX, x_body, 0)

    def y_store(to, cons):
        plus, minus = split_flux(cons, 2, alphas[1])
        for v in range(NV):
            yp[v, to] = plus[v]
            ym[v, to] = minus[v]

    def y_body(i, carry):
        y_store(i + HALO, [state_ref[v, pl.ds(i, CX, stride=CY), :] for v in range(NV)])
        return carry

    lax.fori_loop(0, CY, y_body, 0)
    for i in range(HALO):
        wall = [state_ref[v, pl.ds(i, CX, stride=CY), :] for v in range(NV)]
        wall[2] = -wall[2]
        y_store(HALO - 1 - i, wall)
        y_store(HALO + CY + i, [top_ref[v, i] for v in range(NV)])

    for v in range(NV):
        line[v, :HALO, :] = zlo_ref[v]
        line[v, HALO : HALO + CZ, :] = turned_ref[v]
        line[v, HALO + CZ : 2 * HALO + CZ, :] = zhi_ref[v]

    def z_body(i, carry):
        plus, minus = split_flux([line[v, pl.ds(i, SUB, stride=CZ // SUB), :] for v in range(NV)], 3, alphas[2])
        for v in range(NV):
            zp[v, i] = plus[v]
            zm[v, i] = minus[v]
        return carry

    lax.fori_loop(0, LONG, z_body, 0)

    y_masks = [mask[pl.ds(i, CX, stride=CY), :] > 0.0 for i in range(CY)]
    z_mask = turned_mask > 0.0

    def per_var(v, carry):
        parts = jumps([zp[v, i] for i in range(LONG)], [zm[v, i] for i in range(LONG)], CY, [z_mask] * CY, LAMBDA[2])
        for i in range(CY):
            acc_z[pl.ds(i, SUB, stride=CZ // SUB), :] = parts[i]
        parts = jumps([yp[v, i] for i in range(LONG)], [ym[v, i] for i in range(LONG)], CY, y_masks, LAMBDA[1])
        for i in range(CY):
            acc_y[pl.ds(i, CX, stride=CY), :] = parts[i]
        spread = acc_z[...].T
        for h in range(CY // SUB):
            rows = slice(h * SUB, h * SUB + SUB)
            masks = [mask[i * CY + h * SUB : i * CY + h * SUB + SUB, :] > 0.0 for i in range(CX)]
            parts = jumps(
                [xp[v, i, rows, :] for i in range(WIDE)], [xm[v, i, rows, :] for i in range(WIDE)], CX, masks, LAMBDA[0]
            )
            for i in range(CX):
                at = slice(i * CY + h * SUB, i * CY + h * SUB + SUB)
                change = parts[i] + acc_y[at, :] + spread[at]
                register = REGISTER_DECAY * reg_ref[v, at, :] - change
                new_reg_ref[v, at, :] = register
                new_state_ref[v, at, :] = state_ref[v, at, :] + UPDATE_WEIGHT * register
        return carry

    lax.fori_loop(0, NV, per_var, 0)


def f32(*shape):
    return jax.ShapeDtypeStruct(shape, jnp.float32)


def near(*shape):
    return pltpu.VMEM(shape, jnp.float32)


def held(value):
    return pltpu.with_memory_space_constraint(value, pltpu.VMEM)


def advance(state, register, top_ghost, flags):
    flat = state.reshape(NV, ROWS, CZ)
    halves, n_z = lax.axis_size("gx_0"), lax.axis_size("gz")
    n_plane = lax.axis_size("gx_1") * lax.axis_size("gx_2") * lax.axis_size("gx_3")
    n_x = halves * n_plane

    own = pl.pallas_call(speed_kernel, out_shape=near(halves * n_z, 1, CZ), name="speed")(flat)
    by_line = lax.all_to_all(held(own), ZLINE, 0, 0, tiled=True)
    turned, first, last = pl.pallas_call(
        edges_kernel, out_shape=(near(NV, CZ, ROWS), near(NV, HALO, ROWS), near(NV, HALO, ROWS)), name="edges"
    )(flat)
    relayed = pl.pallas_call(relay_kernel, out_shape=near(n_plane, 1, CZ), name="relay")(held(by_line))
    speeds = lax.all_to_all(held(relayed), PLANE, 0, 0, tiled=True)

    ring = [(i, (i + 1) % n_x) for i in range(n_x)]
    seam = [pair for pair in ring if pair[0] % n_plane == n_plane - 1]
    rest = [pair for pair in ring if pair not in seam]

    def back(pairs):
        return [(b, a) for a, b in pairs]

    upper, lower = state[:, CX - HALO :], state[:, :HALO]
    xlo_seam = lax.ppermute(upper, GX, seam)
    xhi_seam = lax.ppermute(lower, GX, back(seam))
    xlo = lax.ppermute(upper, GX, rest)
    xhi = lax.ppermute(lower, GX, back(rest))
    z_ring = [(i, (i + 1) % n_z) for i in range(n_z)]
    zlo = lax.ppermute(last, "gz", z_ring)
    zhi = lax.ppermute(first, "gz", back(z_ring))

    new_state, new_register = pl.pallas_call(
        step_kernel,
        out_shape=(f32(NV, ROWS, CZ), f32(NV, ROWS, CZ)),
        scratch_shapes=[
            pltpu.VMEM((NV, WIDE, CY, CZ), jnp.float32),
            pltpu.VMEM((NV, WIDE, CY, CZ), jnp.float32),
            pltpu.VMEM((NV, LONG, SUB, CZ), jnp.float32),
            pltpu.VMEM((NV, LONG, SUB, CZ), jnp.float32),
            pltpu.VMEM((NV, LONG, SUB, CZ), jnp.float32),
            pltpu.VMEM((NV, LONG, SUB, CZ), jnp.float32),
            pltpu.VMEM((NV, CZ + 8, ROWS), jnp.float32),
            pltpu.VMEM((ROWS, CZ), jnp.float32),
            pltpu.VMEM((ROWS, CZ), jnp.float32),
            pltpu.VMEM((CZ, ROWS), jnp.float32),
        ],
        name="step",
    )(
        held(speeds), flat, held(turned), held(xlo), held(xhi), held(xlo_seam), held(xhi_seam), held(zlo), held(zhi),
        top_ghost.transpose(0, 2, 1, 3), flags.reshape(ROWS, 1), register.reshape(NV, ROWS, CZ),
    )
    return (new_state.reshape(state.shape), new_register.reshape(state.shape))


def solution(mesh):
    finer = Mesh(
        mesh.devices.reshape(2, 8, 4, 2, mesh.shape["gz"]), ("gx_0", "gx_1", "gx_2", "gx_3", "gz")
    )
    placed = P(None, GX, None, "gz")
    return jax.shard_map(
        advance,
        mesh=finer,
        in_specs=(placed, placed, placed, P(GX, None, "gz")),
        out_specs=(placed, placed),
        check_vma=False,
    )
```

time: 114 us -> 80 us (0.70)
  the two profiles are of different devices: /device:TPU:10 before, /device:TPU:2 now
where the time goes in v2:
time: 80 us; the launch traced here: 79.5 us
  starting transfers between devices  31.5 us (39%)
  blocking collectives  25.1 us (31%)
  Pallas kernels  9.67 us (12%)
  waiting for transfers between devices  9.67 us (12%)
  local copies, waits for them, and re-layouts  2.21 us (3%)
    all_to_all x1, blocking collectives, advance(): by_line = lax.all_to_all(held(own), ZLINE, 0, 0, tiled=True)  25.1 us
    all_to_all x1, starting transfers between devices, advance(): speeds = lax.all_to_all(held(relayed), PLANE, 0, 0, tiled=True)  21.4 us
    ppermute x1, waiting for transfers between devices, advance(): zlo = lax.ppermute(last, 'gz', z_ring)  7.9 us
    pallas_call x1, Pallas kernels, advance(): pl.pallas_call(step_kernel, out_shape=(f32(NV, ROWS, CZ), f32(NV, ROWS, C...  6.76 us
    ppermute x1, starting transfers between devices, advance(): zlo = lax.ppermute(last, 'gz', z_ring)  2.46 us
    ppermute x1, starting transfers between devices, advance(): xlo = lax.ppermute(upper, GX, rest)  2.41 us
    ppermute x1, starting transfers between devices, advance(): xhi = lax.ppermute(lower, GX, back(rest))  1.92 us
    ppermute x1, starting transfers between devices, advance(): zhi = lax.ppermute(first, 'gz', back(z_ring))  1.91 us
  transfers between devices with their start and end apart: 7, of which 2 were waited for; matrix products, arithmetic and copies ran while one was open for 2% of the time, Pallas kernels for 4%

profile of v2, /device:TPU:2, one launch (start us, length us, event | category | flops | bytes accessed | tf_op | source)
XLA Modules:
  0.0 79.5 jit_solution(1740557472320316489)
XLA Ops:
  0.6 1.0 %fusion = (f32[5,3,16,128]{3,2,1,0:T(8,128)S(1)}, f32[5,3,16,128]{3,2,1,0:T(8,128)S(1)}) fusion(f32[5,8,16,128]{3,2,1,0:T(8,128)} %param.4), kind=kLoop, calls=%fused_computation | loop fusion | bytes 491520 | tf_op jit(solution)/shard_map/slice | solution.py:271
  1.6 0.7 collective-permute-start.3
  2.3 1.9 %collective-permute-start.1 = (f32[5,3,16,128]{3,2,1,0:T(8,128)S(1)}, f32[5,3,16,128]{3,2,1,0:T(8,128)S(1)}, u32[]{:S(2)}, u32[]{:S(2)}) collective-permute-start(f32[5,3,16,128]{3,2,1,0:T(8,128)S(1)} %get-tuple-element.12), channel_id=1, source_target_pairs={{6,0},{12,6},{18,12},{24,18},{30,24},{36,30},{42,36},{48,42},{54,4... | collective-permute-start | bytes 368648 | tf_op jit(solution)/shard_map/ppermute | solution.py:275
  4.2 0.7 collective-permute-start.2
  4.9 2.4 %collective-permute-start = (f32[5,3,16,128]{3,2,1,0:T(8,128)S(1)}, f32[5,3,16,128]{3,2,1,0:T(8,128)S(1)}, u32[]{:S(2)}, u32[]{:S(2)}) collective-permute-start(f32[5,3,16,128]{3,2,1,0:T(8,128)S(1)} %get-tuple-element.13), channel_id=1, source_target_pairs={{0,6},{6,12},{12,18},{18,24},{24,30},{30,36},{36,42},{42,48},{48,5... | collective-permute-start | bytes 368648 | tf_op jit(solution)/shard_map/ppermute | solution.py:274
  7.3 1.1 %speed.1 = f32[12,1,128]{2,1,0:T(1,128)S(1)} custom-call(f32[5,128,128]{2,1,0:T(8,128)} %bitcast.6), custom_call_target="tpu_custom_call" | custom-call | tf_op jit(solution)/shard_map/speed/pallas_call | solution.py:256
  8.4 25.1 %all_to_all.10.got_ref = f32[12,1,128]{2,1,0:T(1,128)S(1)} all-to-all(f32[12,1,128]{2,1,0:T(1,128)S(1)} %speed.1), channel_id=1, replica_groups=mesh['gx_0'=2,'gx_1'=8,'gx_2'=4,'gx_3'=2,'gz'=6] {'gx_0','gz'}, dimensions={0} | all-to-all | bytes 12288 | tf_op jit(solution)/shard_map/all_to_all | solution.py:257
  33.5 0.6 relay.1
  34.2 21.4 %all-to-all-start.1 = ((f32[64,1,128]{2,1,0:T(1,128)}), f32[64,1,128]{2,1,0:T(1,128)S(1)}, u32[]{:S(2)}, u32[]{:S(2)}) async-start(f32[64,1,128]{2,1,0:T(1,128)} %relay.1), calls=%async_computation.1 | async-start | bytes 65536 | tf_op jit(solution)/shard_map/all_to_all | solution.py:262
  55.6 1.1 %edges.1 = (f32[5,128,128]{2,1,0:T(8,128)S(1)}, f32[5,3,128]{2,1,0:T(4,128)S(1)}, f32[5,3,128]{2,1,0:T(4,128)S(1)}) custom-call(f32[5,128,128]{2,1,0:T(8,128)} %bitcast.7), custom_call_target="tpu_custom_call" | custom-call | tf_op jit(solution)/shard_map/edges/pallas_call | solution.py:258
  56.8 0.0 copy-start
  56.8 2.5 %collective-permute-start.4 = (f32[5,3,128]{2,1,0:T(4,128)S(1)}, f32[5,3,128]{2,1,0:T(4,128)S(1)}, u32[]{:S(2)}, u32[]{:S(2)}) collective-permute-start(f32[5,3,128]{2,1,0:T(4,128)S(1)} %get-tuple-element.8), channel_id=1, source_target_pairs={{0,1},{1,2},{2,3},{3,4},{4,5},{5,0},{6,7},{7,8},{8,9},{9,10},{10,1... | collective-permute-start | bytes 23048 | tf_op jit(solution)/shard_map/ppermute | solution.py:277
  59.3 7.9 %collective-permute-done.4.zlo_ref = f32[5,3,128]{2,1,0:T(4,128)S(1)} collective-permute-done((f32[5,3,128]{2,1,0:T(4,128)S(1)}, f32[5,3,128]{2,1,0:T(4,128)S(1)}, u32[]{:S(2)}, u32[]{:S(2)}) %collective-permute-start.4) | collective-permute-done | bytes 7712 | tf_op jit(solution)/shard_map/ppermute | solution.py:277
  67.2 1.9 %collective-permute-start.5 = (f32[5,3,128]{2,1,0:T(4,128)S(1)}, f32[5,3,128]{2,1,0:T(4,128)S(1)}, u32[]{:S(2)}, u32[]{:S(2)}) collective-permute-start(f32[5,3,128]{2,1,0:T(4,128)S(1)} %get-tuple-element.9), channel_id=1, source_target_pairs={{1,0},{2,1},{3,2},{4,3},{5,4},{0,5},{7,6},{8,7},{9,8},{10,9},{11,1... | collective-permute-start | bytes 23048 | tf_op jit(solution)/shard_map/ppermute | solution.py:278
  69.1 0.5 broadcast.3
  69.6 0.0 copy-done
  69.6 0.7 reduce.3
  70.3 0.7 reshape.24.flag_ref
  71.0 1.8 %collective-permute-done.5.zhi_ref = f32[5,3,128]{2,1,0:T(4,128)S(1)} collective-permute-done((f32[5,3,128]{2,1,0:T(4,128)S(1)}, f32[5,3,128]{2,1,0:T(4,128)S(1)}, u32[]{:S(2)}, u32[]{:S(2)}) %collective-permute-start.5) | collective-permute-done | bytes 7712 | tf_op jit(solution)/shard_map/ppermute | solution.py:278
  72.7 0.0 all-to-all-done.1.speed_ref
  72.7 0.0 collective-permute-done.3.xhi_seam_ref
  72.7 0.0 collective-permute-done.1.xhi_ref
  72.7 0.0 collective-permute-done.2.xlo_seam_ref
  72.7 0.0 collective-permute-done.xlo_ref
  72.8 6.8 %step.1 = (f32[5,128,128]{2,1,0:T(8,128)}, f32[5,128,128]{2,1,0:T(8,128)}) custom-call(f32[64,1,128]{2,1,0:T(1,128)S(1)} %all-to-all-done.1.speed_ref, f32[5,128,128]{2,1,0:T(8,128)} %bitcast.8, f32[5,128,128]{2,1,0:T(8,128)S(1)} %get-tuple-element.7.turned_ref, f32[5,3,16,128]{3,2,1,0:T(8,128)S(1)} %collective-permute-done.xlo_ref, ...), custom_call_target="tpu_custom_call" | custom-call | tf_op jit(solution)/shard_map/step/pallas_call | solution.py:280
Async XLA Ops:
  1.6 71.1 %collective-permute-start.3 = (f32[5,3,16,128]{3,2,1,0:T(8,128)S(1)}, f32[5,3,16,128]{3,2,1,0:T(8,128)S(1)}, u32[]{:S(2)}, u32[]{:S(2)}) collective-permute-start(f32[5,3,16,128]{3,2,1,0:T(8,128)S(1)} %get-tuple-element.12), channel_id=1, source_target_pairs={{384,378},{0,762},{385,379},{1,763},{386,380},{2,764},{387,381},{3... | collective-permute-start | bytes 368648 | tf_op jit(solution)/shard_map/ppermute | solution.py:273
  2.3 70.4 %collective-permute-start.1 = (f32[5,3,16,128]{3,2,1,0:T(8,128)S(1)}, f32[5,3,16,128]{3,2,1,0:T(8,128)S(1)}, u32[]{:S(2)}, u32[]{:S(2)}) collective-permute-start(f32[5,3,16,128]{3,2,1,0:T(8,128)S(1)} %get-tuple-element.12), channel_id=1, source_target_pairs={{6,0},{12,6},{18,12},{24,18},{30,24},{36,30},{42,36},{48,42},{54,4... | collective-permute-start | bytes 368648 | tf_op jit(solution)/shard_map/ppermute | solution.py:275
  4.2 68.5 %collective-permute-start.2 = (f32[5,3,16,128]{3,2,1,0:T(8,128)S(1)}, f32[5,3,16,128]{3,2,1,0:T(8,128)S(1)}, u32[]{:S(2)}, u32[]{:S(2)}) collective-permute-start(f32[5,3,16,128]{3,2,1,0:T(8,128)S(1)} %get-tuple-element.13), channel_id=1, source_target_pairs={{378,384},{762,0},{379,385},{763,1},{380,386},{764,2},{381,387},{7... | collective-permute-start | bytes 368648 | tf_op jit(solution)/shard_map/ppermute | solution.py:272
  4.9 67.8 %collective-permute-start = (f32[5,3,16,128]{3,2,1,0:T(8,128)S(1)}, f32[5,3,16,128]{3,2,1,0:T(8,128)S(1)}, u32[]{:S(2)}, u32[]{:S(2)}) collective-permute-start(f32[5,3,16,128]{3,2,1,0:T(8,128)S(1)} %get-tuple-element.13), channel_id=1, source_target_pairs={{0,6},{6,12},{12,18},{18,24},{24,30},{30,36},{36,42},{42,48},{48,5... | collective-permute-start | bytes 368648 | tf_op jit(solution)/shard_map/ppermute | solution.py:274
  34.2 38.5 %all-to-all-start.1 = ((f32[64,1,128]{2,1,0:T(1,128)}), f32[64,1,128]{2,1,0:T(1,128)S(1)}, u32[]{:S(2)}, u32[]{:S(2)}) async-start(f32[64,1,128]{2,1,0:T(1,128)} %relay.1), calls=%async_computation.1 | async-start | bytes 65536 | tf_op jit(solution)/shard_map/all_to_all | solution.py:262
  56.8 12.8 %copy-start = (s32[8,16,1]{1,2,0:T(1,128)S(1)}, s32[8,16,1]{1,2,0:T(1,128)}, u32[]{:S(2)}) copy-start(s32[8,16,1]{1,2,0:T(1,128)} %param.7) | copy-start | bytes 1540
  56.8 10.4 %collective-permute-start.4 = (f32[5,3,128]{2,1,0:T(4,128)S(1)}, f32[5,3,128]{2,1,0:T(4,128)S(1)}, u32[]{:S(2)}, u32[]{:S(2)}) collective-permute-start(f32[5,3,128]{2,1,0:T(4,128)S(1)} %get-tuple-element.8), channel_id=1, source_target_pairs={{0,1},{1,2},{2,3},{3,4},{4,5},{5,0},{6,7},{7,8},{8,9},{9,10},{10,1... | collective-permute-start | bytes 23048 | tf_op jit(solution)/shard_map/ppermute | solution.py:277
  67.2 5.6 %collective-permute-start.5 = (f32[5,3,128]{2,1,0:T(4,128)S(1)}, f32[5,3,128]{2,1,0:T(4,128)S(1)}, u32[]{:S(2)}, u32[]{:S(2)}) collective-permute-start(f32[5,3,128]{2,1,0:T(4,128)S(1)} %get-tuple-element.9), channel_id=1, source_target_pairs={{1,0},{2,1},{3,2},{4,3},{5,4},{0,5},{7,6},{8,7},{9,8},{10,9},{11,1... | collective-permute-start | bytes 23048 | tf_op jit(solution)/shard_map/ppermute | solution.py:278

commit v3 on v2

v3 whole, which is shorter than its diff:
```python
import jax
import jax.numpy as jnp
from jax import lax
from jax.experimental import pallas as pl
from jax.experimental.pallas import tpu as pltpu
from jax.sharding import Mesh
from jax.sharding import PartitionSpec as P

GX = ("gx_0", "gx_1", "gx_2", "gx_3")
PLANE = ("gx_1", "gx_2", "gx_3")
ZLINE = ("gx_0", "gz")

GAMMA = 1.4
EPS_WENO = 1e-06
LAMBDA = (0.1, 0.15, 0.1)
REGISTER_DECAY = -5.0 / 9.0
UPDATE_WEIGHT = 15.0 / 16.0

NV = 5
CX = 8
CY = 16
CZ = 128
ROWS = CX * CY
HALO = 3
SUB = 8
LONG = 16 + 2 * HALO


def primitives(cons):
    inverse = 1.0 / cons[0]
    vels = [cons[k] * inverse for k in (1, 2, 3)]
    kinetic = cons[1] * vels[0] + cons[2] * vels[1] + cons[3] * vels[2]
    pressure = (GAMMA - 1.0) * (cons[4] - 0.5 * kinetic)
    return inverse, vels, pressure


def fetch(pairs, sems):
    copies = [pltpu.make_async_copy(src, dst, sems.at[i]) for i, (src, dst) in enumerate(pairs)]
    for copy in copies:
        copy.start()
    for copy in copies:
        copy.wait()


def line_neighbours():
    n_z, here = lax.axis_size("gz"), lax.axis_index("gz")
    first = lax.axis_index("gx_0") * n_z
    return first + lax.rem(here + n_z - 1, n_z), first + lax.rem(here + 1, n_z)


def open_kernel(far_ref, state_ref, out_ref, sems):
    fetch([(far_ref.at[v], state_ref.at[v]) for v in range(NV)], sems)
    best = [None] * 3
    for block in range(ROWS // SUB):
        rows = slice(block * SUB, block * SUB + SUB)
        inverse, vels, pressure = primitives([state_ref[v, rows, :] for v in range(NV)])
        sound = jnp.sqrt(GAMMA * pressure * inverse)
        for k in range(3):
            speed = jnp.abs(vels[k]) + sound
            best[k] = speed if block == 0 else jnp.maximum(best[k], speed)
    lane = lax.broadcasted_iota(jnp.int32, (1, CZ), 1)
    packed = jnp.zeros((1, CZ), jnp.float32)
    for k in range(3):
        top = jnp.max(jnp.max(best[k], axis=0, keepdims=True), axis=1, keepdims=True)
        packed = jnp.where(lane == k, top, packed)
    firsts, lasts = [], []
    for v in range(NV):
        turned = state_ref[v].T
        firsts.append(turned[:HALO])
        lasts.append(turned[CZ - HALO :])
    _, after = line_neighbours()
    for to in range(out_ref.shape[0]):
        forward = after == to
        for v in range(NV):
            out_ref[to, v * HALO : v * HALO + HALO, :] = jnp.where(forward, lasts[v], firsts[v])
        out_ref[to, NV * HALO : NV * HALO + 1, :] = packed


def relay_kernel(got_ref, out_ref):
    row = slice(NV * HALO, NV * HALO + 1)
    best = got_ref[0, row, :]
    for i in range(1, got_ref.shape[0]):
        best = jnp.maximum(best, got_ref[i, row, :])
    for to in range(out_ref.shape[0]):
        out_ref[to] = best


def flux_of(cons, var):
    _, vels, pressure = primitives(cons)
    velocity = vels[var - 1]
    flux = [(cons[v] + pressure if v == 4 else cons[v]) * velocity for v in range(NV)]
    flux[var] = flux[var] + pressure
    return flux


def linear_parts(flux, cons, masks, scale):
    count = len(flux) - 2 * HALO

    def face(j):
        inner, outer = flux[j + 2] + flux[j + 3], flux[j + 1] + flux[j + 4]
        central = 37.0 * inner - 8.0 * outer + (flux[j] + flux[j + 5])
        return central, 7.0 * inner - outer, (cons[j + 4] - cons[j + 1]) - 3.0 * (cons[j + 3] - cons[j + 2])

    faces = [face(j) for j in range(count + 1)]
    base, tilt = [], []
    for low, high, mask in zip(faces, faces[1:], masks):
        base.append(jnp.where(mask, (scale / 12.0) * (high[1] - low[1]), (scale / 60.0) * (high[0] - low[0])))
        tilt.append(jnp.where(mask, (scale / 12.0) * (high[2] - low[2]), 0.0))
    return base, tilt


EPS_SCALED = 16.0 * EPS_WENO
CURVE = 13.0 / 3.0


def bent_faces(flux, cons, alpha):
    count = len(flux) - 2 * HALO + 1
    moved = [alpha * u for u in cons]

    def slopes(vals):
        step = [b - a for a, b in zip(vals, vals[1:])]
        bend = [None] + [b - a for a, b in zip(step, step[1:])]
        turn = [None] + [b - a for a, b in zip(bend[1:], bend[2:])]
        base = [None] + [CURVE * (d * d) + EPS_SCALED for d in bend[1:]]
        return step, bend, turn, base

    def pull(beta_a, beta_b, beta_c, near_turn, far_turn):
        u, w = beta_b / beta_a, beta_b / beta_c
        u, w = u * u, w * w
        w = 3.0 * w
        return ((u + u) * near_turn + w * far_turn) / (6.0 + u + w)

    pe, pd, pt, pk = slopes([f + m for f, m in zip(flux, moved)])
    me, md, mt, mk = slopes([f - m for f, m in zip(flux, moved)])
    out = []
    for j in range(count):
        bc, cd = pe[j + 1], pe[j + 2]
        ta, tb, tc = pd[j + 1] + (bc + bc), bc + cd, pd[j + 3] - (cd + cd)
        plus = pull(pk[j + 1] + ta * ta, pk[j + 2] + tb * tb, pk[j + 3] + tc * tc, pt[j + 1], pt[j + 2])
        bc, cd = me[j + 3], me[j + 2]
        ta, tb, tc = md[j + 4] - (bc + bc), bc + cd, md[j + 2] + (cd + cd)
        minus = pull(mk[j + 4] + ta * ta, mk[j + 3] + tb * tb, mk[j + 2] + tc * tc, mt[j + 3], mt[j + 2])
        out.append(minus - plus)
    return out


def prepare_kernel(
    state_ref, top_ref, flag_ref, yu_ref, ybase_ref, ytilt_ref, xmask_ref, zmask_ref, yf_ref
):
    square = (CY, CY)
    diagonal = lax.broadcasted_iota(jnp.int32, square, 0) == lax.broadcasted_iota(jnp.int32, square, 1)
    for x in range(CX):
        spread = jnp.broadcast_to(flag_ref[x].astype(jnp.float32), square)
        column = jnp.max(jnp.where(diagonal, spread, 0.0), axis=1, keepdims=True)
        xmask_ref[x * CY : x * CY + CY, :] = jnp.broadcast_to(column, (CY, CZ)) * (LAMBDA[0] / 12.0)
    zmask_ref[...] = xmask_ref[...].T[:SUB] * (LAMBDA[2] / LAMBDA[0])

    def y_store(to, cons):
        flux = flux_of(cons, 2)
        for v in range(NV):
            yf_ref[v, to] = flux[v]
            yu_ref[v, to] = cons[v]

    for i in range(CY):
        cons = [state_ref[v, pl.ds(i, CX, stride=CY), :] for v in range(NV)]
        y_store(i + HALO, cons)
        if i < HALO:
            y_store(HALO - 1 - i, [-c if v == 2 else c for v, c in enumerate(cons)])
            y_store(HALO + CY + i, [top_ref[v, i] for v in range(NV)])

    masks = [xmask_ref[pl.ds(i, CX, stride=CY), :] > 0.0 for i in range(CY)]

    def per_var(v, carry):
        planes = range(LONG)
        base, tilt = linear_parts([yf_ref[v, i] for i in planes], [yu_ref[v, i] for i in planes], masks, LAMBDA[1])
        for i in range(CY):
            ybase_ref[v, i] = base[i]
            ytilt_ref[v, i] = tilt[i]
        return carry

    lax.fori_loop(0, NV, per_var, 0)


def z_kernel(got_ref, state_ref, zmask_ref, zu_ref, zbase_ref, ztilt_ref, zf_ref, line):
    before, after = line_neighbours()
    for v in range(NV):
        rows = slice(v * HALO, v * HALO + HALO)
        line[v, :HALO, :] = got_ref[before, rows, :]
        line[v, HALO : HALO + CZ, :] = state_ref[v].T
        line[v, HALO + CZ : 2 * HALO + CZ, :] = got_ref[after, rows, :]
    for i in range(LONG):
        cons = [line[v, pl.ds(i, SUB, stride=CZ // SUB), :] for v in range(NV)]
        flux = flux_of(cons, 3)
        for v in range(NV):
            zf_ref[v, i] = flux[v]
            zu_ref[v, i] = cons[v]
    mask = zmask_ref[...] > 0.0

    def per_var(v, carry):
        planes = range(LONG)
        base, tilt = linear_parts(
            [zf_ref[v, i] for i in planes], [zu_ref[v, i] for i in planes], [mask] * CY, LAMBDA[2]
        )
        for i in range(CY):
            zbase_ref[v, i] = base[i]
            ztilt_ref[v, i] = tilt[i]
        return carry

    lax.fori_loop(0, NV, per_var, 0)


def step_kernel(
    speed_ref, state_ref, xlo_ref, xhi_ref, xlo_seam_ref, xhi_seam_ref,
    yu_ref, ybase_ref, ytilt_ref, zu_ref, zbase_ref, ztilt_ref, xmask_ref, zmask_ref, old_reg_ref,
    far_state_ref, far_reg_ref,
    ymask_ref, xf_ref, yf_ref, zf_ref, side_f, side_u, acc_y, acc_z, reg_ref, state_out, reg_out, sems,
):
    loads = [pltpu.make_async_copy(old_reg_ref.at[v], reg_ref.at[v], sems.at[2, v]) for v in range(NV)]
    for load in loads:
        load.start()

    best = speed_ref[0]
    for i in range(1, speed_ref.shape[0]):
        best = jnp.maximum(best, speed_ref[i])
    lane = lax.broadcasted_iota(jnp.int32, (1, CZ), 1)
    alphas = [jnp.max(jnp.where(lane == k, best, 0.0), axis=1, keepdims=True) for k in range(3)]
    halves = [slice(h * SUB, h * SUB + SUB) for h in range(CY // SUB)]

    for i in range(HALO):
        for rows in halves:
            for at, rest, seam in ((i, xlo_ref, xlo_seam_ref), (HALO + i, xhi_ref, xhi_seam_ref)):
                cons = [rest[v, i, rows, :] + seam[v, i, rows, :] for v in range(NV)]
                flux = flux_of(cons, 1)
                for v in range(NV):
                    side_f[v, at, rows, :] = flux[v]
                    side_u[v, at, rows, :] = cons[v]

    for i in range(LONG):
        for cons_ref, flux_ref, var in ((yu_ref, yf_ref, 2), (zu_ref, zf_ref, 3)):
            flux = flux_of([cons_ref[v, i] for v in range(NV)], var)
            for v in range(NV):
                flux_ref[v, i] = flux[v]
    for block in range(ROWS // SUB):
        rows = slice(block * SUB, block * SUB + SUB)
        flux = flux_of([state_ref[v, rows, :] for v in range(NV)], 1)
        for v in range(NV):
            xf_ref[v, rows, :] = flux[v]
    for y in range(CY):
        ymask_ref[y] = xmask_ref[pl.ds(y, CX, stride=CY), :] * (LAMBDA[1] / LAMBDA[0])
    for load in loads:
        load.wait()

    def copies(v):
        return [
            pltpu.make_async_copy(state_out.at[v], far_state_ref.at[v], sems.at[0, v]),
            pltpu.make_async_copy(reg_out.at[v], far_reg_ref.at[v], sems.at[1, v]),
        ]

    def per_var(v, carry):
        bent = bent_faces([zf_ref[v, i] for i in range(LONG)], [zu_ref[v, i] for i in range(LONG)], alphas[2])
        for i in range(CY):
            acc_z[pl.ds(i, SUB, stride=CZ // SUB), :] = (
                zbase_ref[v, i] + alphas[2] * ztilt_ref[v, i] + zmask_ref[...] * (bent[i + 1] - bent[i])
            )
        bent = bent_faces([yf_ref[v, i] for i in range(LONG)], [yu_ref[v, i] for i in range(LONG)], alphas[1])
        for i in range(CY):
            acc_y[pl.ds(i, CX, stride=CY), :] = (
                ybase_ref[v, i] + alphas[1] * ytilt_ref[v, i] + ymask_ref[i] * (bent[i + 1] - bent[i])
            )
        spread = acc_z[...].T
        for rows in halves:
            at = [slice(i * CY + rows.start, i * CY + rows.stop) for i in range(CX)]
            flux = (
                [side_f[v, i, rows, :] for i in range(HALO)]
                + [xf_ref[v, here, :] for here in at]
                + [side_f[v, HALO + i, rows, :] for i in range(HALO)]
            )
            cons = (
                [side_u[v, i, rows, :] for i in range(HALO)]
                + [state_ref[v, here, :] for here in at]
                + [side_u[v, HALO + i, rows, :] for i in range(HALO)]
            )
            bent = bent_faces(flux, cons, alphas[0])
            base, tilt = linear_parts(flux, cons, [xmask_ref[here, :] > 0.0 for here in at], LAMBDA[0])
            for i, here in enumerate(at):
                x_part = base[i] + alphas[0] * tilt[i] + xmask_ref[here, :] * (bent[i + 1] - bent[i])
                change = x_part + acc_y[here, :] + spread[here]
                register = REGISTER_DECAY * reg_ref[v, here, :] - change
                reg_out[v, here, :] = register
                state_out[v, here, :] = state_ref[v, here, :] + UPDATE_WEIGHT * register
        for copy in copies(v):
            copy.start()
        return carry

    lax.fori_loop(0, NV, per_var, 0)
    for v in range(NV):
        for copy in copies(v):
            copy.wait()


def f32(*shape):
    return jax.ShapeDtypeStruct(shape, jnp.float32)


def near(*shape):
    return pltpu.VMEM(shape, jnp.float32)


ROOM = pltpu.CompilerParams(vmem_limit_bytes=16 * 1024 * 1024)


def held(value):
    return pltpu.with_memory_space_constraint(value, pltpu.VMEM)


def afar(value):
    return pltpu.with_memory_space_constraint(value, pltpu.HBM)


def advance(state, register, top_ghost, flags):
    flat = state.reshape(NV, ROWS, CZ)
    halves, n_z = lax.axis_size("gx_0"), lax.axis_size("gz")
    n_plane = lax.axis_size("gx_1") * lax.axis_size("gx_2") * lax.axis_size("gx_3")
    n_x = halves * n_plane

    far = pl.BlockSpec(memory_space=pltpu.HBM)
    close = pl.BlockSpec(memory_space=pltpu.VMEM)
    planes, strips = (NV, LONG, SUB, CZ), (NV, CY, SUB, CZ)
    near_state, own = pl.pallas_call(
        open_kernel,
        in_specs=[far],
        out_shape=(near(NV, ROWS, CZ), near(halves * n_z, NV * HALO + 1, CZ)),
        scratch_shapes=[pltpu.SemaphoreType.DMA((NV,))],
        compiler_params=ROOM, name="open",
    )(afar(flat))
    by_line = lax.all_to_all(held(own), ZLINE, 0, 0, tiled=True)
    yu, ybase, ytilt, xmask, zmask = pl.pallas_call(
        prepare_kernel,
        out_shape=(
            near(*planes), near(*strips), near(*strips), near(ROWS, CZ), near(SUB, ROWS),
        ),
        scratch_shapes=[pltpu.VMEM(planes, jnp.float32)],
        compiler_params=ROOM, name="prepare",
    )(held(near_state), top_ghost.transpose(0, 2, 1, 3), flags.transpose(0, 2, 1))
    relayed = pl.pallas_call(relay_kernel, out_shape=near(n_plane, 1, CZ), compiler_params=ROOM, name="relay")(held(by_line))
    speeds = lax.all_to_all(held(relayed), PLANE, 0, 0, tiled=True)
    zu, zbase, ztilt = pl.pallas_call(
        z_kernel,
        out_shape=(near(*planes), near(*strips), near(*strips)),
        scratch_shapes=[pltpu.VMEM(planes, jnp.float32), pltpu.VMEM((NV, CZ + 8, ROWS), jnp.float32)],
        compiler_params=ROOM, name="z_prepare",
    )(held(by_line), held(near_state), held(zmask))

    ring = [(i, (i + 1) % n_x) for i in range(n_x)]
    seam = [pair for pair in ring if pair[0] % n_plane == n_plane - 1]
    rest = [pair for pair in ring if pair not in seam]

    def back(pairs):
        return [(b, a) for a, b in pairs]

    blocks = near_state.reshape(state.shape)
    upper, lower = blocks[:, CX - HALO :], blocks[:, :HALO]
    xlo_seam = lax.ppermute(upper, GX, seam)
    xhi_seam = lax.ppermute(lower, GX, back(seam))
    xlo = lax.ppermute(upper, GX, rest)
    xhi = lax.ppermute(lower, GX, back(rest))

    new_state, new_register = pl.pallas_call(
        step_kernel,
        out_shape=(f32(NV, ROWS, CZ), f32(NV, ROWS, CZ)),
        in_specs=[close] * 14 + [far],
        out_specs=(far, far),
        scratch_shapes=[
            pltpu.VMEM((CY, CX, CZ), jnp.float32),
            pltpu.VMEM((NV, ROWS, CZ), jnp.float32),
            pltpu.VMEM(planes, jnp.float32),
            pltpu.VMEM(planes, jnp.float32),
            pltpu.VMEM((NV, 2 * HALO, CY, CZ), jnp.float32),
            pltpu.VMEM((NV, 2 * HALO, CY, CZ), jnp.float32),
            pltpu.VMEM((ROWS, CZ), jnp.float32),
            pltpu.VMEM((CZ, ROWS), jnp.float32),
            pltpu.VMEM((NV, ROWS, CZ), jnp.float32),
            pltpu.VMEM((NV, ROWS, CZ), jnp.float32),
            pltpu.VMEM((NV, ROWS, CZ), jnp.float32),
            pltpu.SemaphoreType.DMA((3, NV)),
        ],
        compiler_params=ROOM, name="step",
    )(
        *map(held, (
            speeds, near_state, xlo, xhi, xlo_seam, xhi_seam,
            yu, ybase, ytilt, zu, zbase, ztilt, xmask, zmask,
        )),
        afar(register.reshape(NV, ROWS, CZ)),
    )
    return (new_state.reshape(state.shape), new_register.reshape(state.shape))


def solution(mesh):
    finer = Mesh(
        mesh.devices.reshape(2, 8, 4, 2, mesh.shape["gz"]), ("gx_0", "gx_1", "gx_2", "gx_3", "gz")
    )
    placed = P(None, GX, None, "gz")
    return jax.shard_map(
        advance,
        mesh=finer,
        in_specs=(placed, placed, placed, P(GX, None, "gz")),
        out_specs=(placed, placed),
        check_vma=False,
    )
```

time: 80 us -> 61 us (0.76)
  the two profiles are of different devices: /device:TPU:2 before, /device:TPU:1 now
where the time goes in v3:
time: 61 us; the launch traced here: 60.5 us
  starting transfers between devices  43.1 us (71%)
  Pallas kernels  8.42 us (14%)
  waiting for transfers between devices  8.19 us (13%)
  between operations  0.76 us (1%)
    ppermute x1, starting transfers between devices, advance(): xhi = lax.ppermute(lower, GX, back(rest))  16.4 us
    all_to_all x1, starting transfers between devices, advance(): by_line = lax.all_to_all(held(own), ZLINE, 0, 0, tiled=True)  15.7 us
    all_to_all x1, waiting for transfers between devices, advance(): speeds = lax.all_to_all(held(relayed), PLANE, 0, 0, tiled=True)  8.18 us
    all_to_all x1, starting transfers between devices, advance(): speeds = lax.all_to_all(held(relayed), PLANE, 0, 0, tiled=True)  7.8 us
    pallas_call x1, Pallas kernels, advance(): pl.pallas_call(step_kernel, out_shape=(f32(NV, ROWS, CZ), f32(NV, ROWS, C...  4.77 us
    pallas_call x1, Pallas kernels, advance(): pl.pallas_call(open_kernel, in_specs=[far], out_shape=(near(NV, ROWS, CZ)...  1.92 us
    ppermute x1, starting transfers between devices, advance(): xlo = lax.ppermute(upper, GX, rest)  1.92 us
  transfers between devices with their start and end apart: 6, of which 1 were waited for; matrix products, arithmetic and copies ran while one was open for 0% of the time, Pallas kernels for 3%

profile of v3, /device:TPU:1, one launch (start us, length us, event | category | flops | bytes accessed | tf_op | source)
XLA Modules:
  0.0 60.5 jit_solution(2636343969556231668)
XLA Ops:
  0.6 1.9 %open.1 = (f32[5,128,128]{2,1,0:T(8,128)S(1)}, f32[12,16,128]{2,1,0:T(8,128)}) custom-call(f32[5,128,128]{2,1,0:T(8,128)} %bitcast.12), custom_call_target="tpu_custom_call" | custom-call | tf_op jit(solution)/shard_map/open/pallas_call | solution.py:329
  2.6 15.7 %all-to-all-start = ((f32[12,16,128]{2,1,0:T(8,128)}), f32[12,16,128]{2,1,0:T(8,128)S(1)}, u32[]{:S(2)}, u32[]{:S(2)}) async-start(f32[12,16,128]{2,1,0:T(8,128)} %get-tuple-element.14), calls=%async_computation | async-start | bytes 196608 | tf_op jit(solution)/shard_map/all_to_all | solution.py:336
  18.3 0.7 %collective-permute-start.3 = (f32[5,3,16,128]{3,2,1,0:T(8,128)S(1)}, f32[5,3,16,128]{3,2,1,0:T(8,128)S(1)}, u32[]{:S(2)}, u32[]{:S(2)}) collective-permute-start(f32[5,3,16,128]{3,2,1,0:T(8,128)S(1)} %get-tuple-element.26), channel_id=1, source_target_pairs={{384,378},{0,762},{385,379},{1,763},{386,380},{2,764},{387,381},{3... | collective-permute-start | bytes 368648 | tf_op jit(solution)/shard_map/ppermute | solution.py:364
  19.0 16.4 %collective-permute-start.1 = (f32[5,3,16,128]{3,2,1,0:T(8,128)S(1)}, f32[5,3,16,128]{3,2,1,0:T(8,128)S(1)}, u32[]{:S(2)}, u32[]{:S(2)}) collective-permute-start(f32[5,3,16,128]{3,2,1,0:T(8,128)S(1)} %get-tuple-element.26), channel_id=1, source_target_pairs={{6,0},{12,6},{18,12},{24,18},{30,24},{36,30},{42,36},{48,42},{54,4... | collective-permute-start | bytes 368648 | tf_op jit(solution)/shard_map/ppermute | solution.py:366
  35.4 0.7 %collective-permute-start.2 = (f32[5,3,16,128]{3,2,1,0:T(8,128)S(1)}, f32[5,3,16,128]{3,2,1,0:T(8,128)S(1)}, u32[]{:S(2)}, u32[]{:S(2)}) collective-permute-start(f32[5,3,16,128]{3,2,1,0:T(8,128)S(1)} %get-tuple-element.27), channel_id=1, source_target_pairs={{378,384},{762,0},{379,385},{763,1},{380,386},{764,2},{381,387},{7... | collective-permute-start | bytes 368648 | tf_op jit(solution)/shard_map/ppermute | solution.py:363
  36.0 1.9 %collective-permute-start = (f32[5,3,16,128]{3,2,1,0:T(8,128)S(1)}, f32[5,3,16,128]{3,2,1,0:T(8,128)S(1)}, u32[]{:S(2)}, u32[]{:S(2)}) collective-permute-start(f32[5,3,16,128]{3,2,1,0:T(8,128)S(1)} %get-tuple-element.27), channel_id=1, source_target_pairs={{0,6},{6,12},{12,18},{18,24},{24,30},{30,36},{36,42},{42,48},{48,5... | collective-permute-start | bytes 368648 | tf_op jit(solution)/shard_map/ppermute | solution.py:365
  38.0 0.0 all-to-all-done.got_ref
  38.0 0.6 %relay.1 = f32[64,1,128]{2,1,0:T(1,128)} custom-call(f32[12,16,128]{2,1,0:T(8,128)S(1)} %all-to-all-done.got_ref), custom_call_target="tpu_custom_call" | custom-call | tf_op jit(solution)/shard_map/relay/pallas_call | solution.py:345
  38.6 0.0 copy-start
  38.6 0.0 copy-start.1
  38.6 7.8 %all-to-all-start.1 = ((f32[64,1,128]{2,1,0:T(1,128)}), f32[64,1,128]{2,1,0:T(1,128)S(1)}, u32[]{:S(2)}, u32[]{:S(2)}) async-start(f32[64,1,128]{2,1,0:T(1,128)} %relay.1), calls=%async_computation.1 | async-start | bytes 65536 | tf_op jit(solution)/shard_map/all_to_all | solution.py:346
  46.4 0.0 copy-done
  46.4 0.0 copy-done.1
  46.5 0.5 prepare.1
  47.0 0.6 z_prepare.1
  47.5 0.0 collective-permute-done.3.xhi_seam_ref
  47.6 0.0 collective-permute-done.1.xhi_ref
  47.6 0.0 collective-permute-done.2.xlo_seam_ref
  47.6 0.0 collective-permute-done.xlo_ref
  47.6 8.2 %all-to-all-done.1.speed_ref = f32[64,1,128]{2,1,0:T(1,128)S(1)} async-done(((f32[64,1,128]{2,1,0:T(1,128)}), f32[64,1,128]{2,1,0:T(1,128)S(1)}, u32[]{:S(2)}, u32[]{:S(2)}) %all-to-all-start.1) | async-done | bytes 32800 | tf_op jit(solution)/shard_map/all_to_all | solution.py:346
  55.8 4.8 %step.1 = (f32[5,128,128]{2,1,0:T(8,128)}, f32[5,128,128]{2,1,0:T(8,128)}) custom-call(f32[64,1,128]{2,1,0:T(1,128)S(1)} %all-to-all-done.1.speed_ref, f32[5,128,128]{2,1,0:T(8,128)S(1)} %get-tuple-element.15.state_ref, f32[5,3,16,128]{3,2,1,0:T(8,128)S(1)} %collective-permute-done.xlo_ref, f32[5,3,16,128]{3,2,1,0:T(8,128)S(1)} %collective-permute-done.1.xhi_ref, ...), custom_call_target="tpu_custom_call" | custom-call | tf_op jit(solution)/shard_map/step/pallas_call | solution.py:368
  (1 shorter events, 0.0 us)
Async XLA Ops:
  2.6 35.4 %all-to-all-start = ((f32[12,16,128]{2,1,0:T(8,128)}), f32[12,16,128]{2,1,0:T(8,128)S(1)}, u32[]{:S(2)}, u32[]{:S(2)}) async-start(f32[12,16,128]{2,1,0:T(8,128)} %get-tuple-element.14), calls=%async_computation | async-start | bytes 196608 | tf_op jit(solution)/shard_map/all_to_all | solution.py:336
  18.3 29.2 %collective-permute-start.3 = (f32[5,3,16,128]{3,2,1,0:T(8,128)S(1)}, f32[5,3,16,128]{3,2,1,0:T(8,128)S(1)}, u32[]{:S(2)}, u32[]{:S(2)}) collective-permute-start(f32[5,3,16,128]{3,2,1,0:T(8,128)S(1)} %get-tuple-element.26), channel_id=1, source_target_pairs={{384,378},{0,762},{385,379},{1,763},{386,380},{2,764},{387,381},{3... | collective-permute-start | bytes 368648 | tf_op jit(solution)/shard_map/ppermute | solution.py:364
  19.0 28.6 %collective-permute-start.1 = (f32[5,3,16,128]{3,2,1,0:T(8,128)S(1)}, f32[5,3,16,128]{3,2,1,0:T(8,128)S(1)}, u32[]{:S(2)}, u32[]{:S(2)}) collective-permute-start(f32[5,3,16,128]{3,2,1,0:T(8,128)S(1)} %get-tuple-element.26), channel_id=1, source_target_pairs={{6,0},{12,6},{18,12},{24,18},{30,24},{36,30},{42,36},{48,42},{54,4... | collective-permute-start | bytes 368648 | tf_op jit(solution)/shard_map/ppermute | solution.py:366
  35.4 12.2 %collective-permute-start.2 = (f32[5,3,16,128]{3,2,1,0:T(8,128)S(1)}, f32[5,3,16,128]{3,2,1,0:T(8,128)S(1)}, u32[]{:S(2)}, u32[]{:S(2)}) collective-permute-start(f32[5,3,16,128]{3,2,1,0:T(8,128)S(1)} %get-tuple-element.27), channel_id=1, source_target_pairs={{378,384},{762,0},{379,385},{763,1},{380,386},{764,2},{381,387},{7... | collective-permute-start | bytes 368648 | tf_op jit(solution)/shard_map/ppermute | solution.py:363
  36.0 11.5 %collective-permute-start = (f32[5,3,16,128]{3,2,1,0:T(8,128)S(1)}, f32[5,3,16,128]{3,2,1,0:T(8,128)S(1)}, u32[]{:S(2)}, u32[]{:S(2)}) collective-permute-start(f32[5,3,16,128]{3,2,1,0:T(8,128)S(1)} %get-tuple-element.27), channel_id=1, source_target_pairs={{0,6},{6,12},{12,18},{18,24},{24,30},{30,36},{36,42},{42,48},{48,5... | collective-permute-start | bytes 368648 | tf_op jit(solution)/shard_map/ppermute | solution.py:365
  38.6 7.8 %copy-start = (f32[5,8,3,128]{3,1,2,0:T(8,128)S(1)}, f32[5,8,3,128]{3,1,2,0:T(8,128)}, u32[]{:S(2)}) copy-start(f32[5,8,3,128]{3,1,2,0:T(8,128)} %param.6) | copy-start | bytes 184324
  38.6 7.8 %copy-start.1 = (s32[8,16,1]{1,2,0:T(1,128)S(1)}, s32[8,16,1]{1,2,0:T(1,128)}, u32[]{:S(2)}) copy-start(s32[8,16,1]{1,2,0:T(1,128)} %param.7) | copy-start | bytes 1540
  38.6 17.1 %all-to-all-start.1 = ((f32[64,1,128]{2,1,0:T(1,128)}), f32[64,1,128]{2,1,0:T(1,128)S(1)}, u32[]{:S(2)}, u32[]{:S(2)}) async-start(f32[64,1,128]{2,1,0:T(1,128)} %relay.1), calls=%async_computation.1 | async-start | bytes 65536 | tf_op jit(solution)/shard_map/all_to_all | solution.py:346

commit v4 on v3

--- a/solution.py
+++ b/solution.py
@@ -321,7 +321,6 @@
     flat = state.reshape(NV, ROWS, CZ)
     halves, n_z = lax.axis_size("gx_0"), lax.axis_size("gz")
     n_plane = lax.axis_size("gx_1") * lax.axis_size("gx_2") * lax.axis_size("gx_3")
-    n_x = halves * n_plane
 
     far = pl.BlockSpec(memory_space=pltpu.HBM)
     close = pl.BlockSpec(memory_space=pltpu.VMEM)
@@ -351,19 +350,18 @@
         compiler_params=ROOM, name="z_prepare",
     )(held(by_line), held(near_state), held(zmask))
 
-    ring = [(i, (i + 1) % n_x) for i in range(n_x)]
-    seam = [pair for pair in ring if pair[0] % n_plane == n_plane - 1]
-    rest = [pair for pair in ring if pair not in seam]
-
-    def back(pairs):
-        return [(b, a) for a, b in pairs]
+    ahead = [(i, i + 1) for i in range(n_plane - 1)]
+    lows = [((h + 1) % halves * n_plane, h * n_plane) for h in range(halves)]
+    highs = [(h * n_plane + n_plane - 1, (h + 1) % halves * n_plane + n_plane - 1) for h in range(halves)]
 
     blocks = near_state.reshape(state.shape)
     upper, lower = blocks[:, CX - HALO :], blocks[:, :HALO]
-    xlo_seam = lax.ppermute(upper, GX, seam)
-    xhi_seam = lax.ppermute(lower, GX, back(seam))
-    xlo = lax.ppermute(upper, GX, rest)
-    xhi = lax.ppermute(lower, GX, back(rest))
+    xhi = lax.ppermute(lower, PLANE, [(b, a) for a, b in ahead])
+    low_end = lax.ppermute(lower, GX, lows)
+    high_end = lax.ppermute(upper, GX, highs)
+    xlo = lax.ppermute(upper, PLANE, ahead)
+    xhi_seam = lax.ppermute(low_end, PLANE, [(0, n_plane - 1)])
+    xlo_seam = lax.ppermute(high_end, PLANE, [(n_plane - 1, 0)])
 
     new_state, new_register = pl.pallas_call(
         step_kernel,

time: 61 us -> 63.8 us (1.046)
  starting transfers between devices: 43.1 us -> 45.9 us
    all_to_all x1, starting transfers between devices: 7.8 us -> 12.5 us  [advance(): speeds = lax.all_to_all(held(relayed), PLANE, 0, 0, tiled=True)]
    ppermute x4 -> x6, starting transfers between devices: 19.6 us -> 17.6 us  [the longest x1 11.8 us: advance(): xhi = lax.ppermute(lower, PLANE, [(b, a) for a, b in ahead])]
  transfers between devices with their start and end apart: 6 -> 8, of which waited for: 1 -> 1; matrix products, arithmetic and copies ran while one was open for 0% -> 0% of each run, Pallas kernels for 3% -> 3%
where the time goes in v4:
time: 63.8 us; the launch traced here: 63.3 us
  starting transfers between devices  45.9 us (72%)
  Pallas kernels  8.42 us (13%)
  waiting for transfers between devices  8.19 us (13%)
  between operations  0.78 us (1%)
    all_to_all x1, starting transfers between devices, advance(): by_line = lax.all_to_all(held(own), ZLINE, 0, 0, tiled=True)  15.7 us
    all_to_all x1, starting transfers between devices, advance(): speeds = lax.all_to_all(held(relayed), PLANE, 0, 0, tiled=True)  12.5 us
    ppermute x1, starting transfers between devices, advance(): xhi = lax.ppermute(lower, PLANE, [(b, a) for a, b in ahead])  11.8 us
    all_to_all x1, waiting for transfers between devices, advance(): speeds = lax.all_to_all(held(relayed), PLANE, 0, 0, tiled=True)  8.18 us
    pallas_call x1, Pallas kernels, advance(): pl.pallas_call(step_kernel, out_shape=(f32(NV, ROWS, CZ), f32(NV, ROWS, C...  4.77 us
    pallas_call x1, Pallas kernels, advance(): pl.pallas_call(open_kernel, in_specs=[far], out_shape=(near(NV, ROWS, CZ)...  1.92 us
    ppermute x1, starting transfers between devices, advance(): xlo = lax.ppermute(upper, PLANE, ahead)  1.92 us
    ppermute x1, starting transfers between devices, advance(): high_end = lax.ppermute(upper, GX, highs)  1.31 us
  transfers between devices with their start and end apart: 8, of which 1 were waited for; matrix products, arithmetic and copies ran while one was open for 0% of the time, Pallas kernels for 3%

profile of v4, /device:TPU:1, one launch (start us, length us, event | category | flops | bytes accessed | tf_op | source)
XLA Modules:
  0.0 63.3 jit_solution(5273087867717906115)
XLA Ops:
  0.6 1.9 %open.1 = (f32[5,128,128]{2,1,0:T(8,128)S(1)}, f32[12,16,128]{2,1,0:T(8,128)}) custom-call(f32[5,128,128]{2,1,0:T(8,128)} %bitcast.12), custom_call_target="tpu_custom_call" | custom-call | tf_op jit(solution)/shard_map/open/pallas_call | solution.py:328
  2.6 15.7 %all-to-all-start = ((f32[12,16,128]{2,1,0:T(8,128)}), f32[12,16,128]{2,1,0:T(8,128)S(1)}, u32[]{:S(2)}, u32[]{:S(2)}) async-start(f32[12,16,128]{2,1,0:T(8,128)} %get-tuple-element.14), calls=%async_computation | async-start | bytes 196608 | tf_op jit(solution)/shard_map/all_to_all | solution.py:335
  18.3 1.3 %collective-permute-start.4 = (f32[5,3,16,128]{3,2,1,0:T(8,128)S(1)}, f32[5,3,16,128]{3,2,1,0:T(8,128)}, u32[]{:S(2)}, u32[]{:S(2)}) collective-permute-start(f32[5,3,16,128]{3,2,1,0:T(8,128)S(1)} %get-tuple-element.26), channel_id=1, source_target_pairs={{384,0},{0,384},{385,1},{1,385},{386,2},{2,386},{387,3},{3,387},{3... | collective-permute-start | bytes 368648 | tf_op jit(solution)/shard_map/ppermute | solution.py:360
  19.6 1.3 %collective-permute-start.2 = (f32[5,3,16,128]{3,2,1,0:T(8,128)S(1)}, f32[5,3,16,128]{3,2,1,0:T(8,128)}, u32[]{:S(2)}, u32[]{:S(2)}) collective-permute-start(f32[5,3,16,128]{3,2,1,0:T(8,128)S(1)} %get-tuple-element.27), channel_id=1, source_target_pairs={{378,762},{762,378},{379,763},{763,379},{380,764},{764,380},{381,7... | collective-permute-start | bytes 368648 | tf_op jit(solution)/shard_map/ppermute | solution.py:361
  20.9 11.8 %collective-permute-start.1 = (f32[5,3,16,128]{3,2,1,0:T(8,128)S(1)}, f32[5,3,16,128]{3,2,1,0:T(8,128)S(1)}, u32[]{:S(2)}, u32[]{:S(2)}) collective-permute-start(f32[5,3,16,128]{3,2,1,0:T(8,128)S(1)} %get-tuple-element.26), channel_id=1, source_target_pairs={{6,0},{12,6},{18,12},{24,18},{30,24},{36,30},{42,36},{48,42},{54,4... | collective-permute-start | bytes 368648 | tf_op jit(solution)/shard_map/ppermute | solution.py:359
  32.7 1.9 %collective-permute-start = (f32[5,3,16,128]{3,2,1,0:T(8,128)S(1)}, f32[5,3,16,128]{3,2,1,0:T(8,128)S(1)}, u32[]{:S(2)}, u32[]{:S(2)}) collective-permute-start(f32[5,3,16,128]{3,2,1,0:T(8,128)S(1)} %get-tuple-element.27), channel_id=1, source_target_pairs={{0,6},{6,12},{12,18},{18,24},{24,30},{30,36},{36,42},{42,48},{48,5... | collective-permute-start | bytes 368648 | tf_op jit(solution)/shard_map/ppermute | solution.py:362
  34.6 0.0 collective-permute-done.4
  34.6 0.7 %collective-permute-start.5 = (f32[5,3,16,128]{3,2,1,0:T(8,128)}, f32[5,3,16,128]{3,2,1,0:T(8,128)S(1)}, u32[]{:S(2)}, u32[]{:S(2)}) collective-permute-start(f32[5,3,16,128]{3,2,1,0:T(8,128)} %collective-permute-done.4), channel_id=1, source_target_pairs={{0,378},{1,379},{2,380},{3,381},{4,382},{5,383},{384,762},{385,763... | collective-permute-start | bytes 368648 | tf_op jit(solution)/shard_map/ppermute | solution.py:363
  35.3 0.0 collective-permute-done.2
  35.3 0.7 %collective-permute-start.3 = (f32[5,3,16,128]{3,2,1,0:T(8,128)}, f32[5,3,16,128]{3,2,1,0:T(8,128)S(1)}, u32[]{:S(2)}, u32[]{:S(2)}) collective-permute-start(f32[5,3,16,128]{3,2,1,0:T(8,128)} %collective-permute-done.2), channel_id=1, source_target_pairs={{378,0},{379,1},{380,2},{381,3},{382,4},{383,5},{762,384},{763,385... | collective-permute-start | bytes 368648 | tf_op jit(solution)/shard_map/ppermute | solution.py:364
  36.0 0.0 all-to-all-done.got_ref
  36.0 0.6 %relay.1 = f32[64,1,128]{2,1,0:T(1,128)} custom-call(f32[12,16,128]{2,1,0:T(8,128)S(1)} %all-to-all-done.got_ref), custom_call_target="tpu_custom_call" | custom-call | tf_op jit(solution)/shard_map/relay/pallas_call | solution.py:344
  36.7 0.0 copy-start
  36.7 0.0 copy-start.1
  36.7 12.5 %all-to-all-start.1 = ((f32[64,1,128]{2,1,0:T(1,128)}), f32[64,1,128]{2,1,0:T(1,128)S(1)}, u32[]{:S(2)}, u32[]{:S(2)}) async-start(f32[64,1,128]{2,1,0:T(1,128)} %relay.1), calls=%async_computation.1 | async-start | bytes 65536 | tf_op jit(solution)/shard_map/all_to_all | solution.py:345
  49.2 0.0 copy-done
  49.2 0.0 copy-done.1
  49.2 0.5 prepare.1
  49.7 0.6 z_prepare.1
  50.3 0.0 collective-permute-done.1.xhi_ref
  50.3 0.0 collective-permute-done.xlo_ref
  50.3 0.0 collective-permute-done.5.xhi_seam_ref
  50.3 0.0 collective-permute-done.3.xlo_seam_ref
  50.3 8.2 %all-to-all-done.1.speed_ref = f32[64,1,128]{2,1,0:T(1,128)S(1)} async-done(((f32[64,1,128]{2,1,0:T(1,128)}), f32[64,1,128]{2,1,0:T(1,128)S(1)}, u32[]{:S(2)}, u32[]{:S(2)}) %all-to-all-start.1) | async-done | bytes 32800 | tf_op jit(solution)/shard_map/all_to_all | solution.py:345
  58.5 4.8 %step.1 = (f32[5,128,128]{2,1,0:T(8,128)}, f32[5,128,128]{2,1,0:T(8,128)}) custom-call(f32[64,1,128]{2,1,0:T(1,128)S(1)} %all-to-all-done.1.speed_ref, f32[5,128,128]{2,1,0:T(8,128)S(1)} %get-tuple-element.15.state_ref, f32[5,3,16,128]{3,2,1,0:T(8,128)S(1)} %collective-permute-done.xlo_ref, f32[5,3,16,128]{3,2,1,0:T(8,128)S(1)} %collective-permute-done.1.xhi_ref, ...), custom_call_target="tpu_custom_call" | custom-call | tf_op jit(solution)/shard_map/step/pallas_call | solution.py:366
  (1 shorter events, 0.0 us)
Async XLA Ops:
  2.6 33.4 %all-to-all-start = ((f32[12,16,128]{2,1,0:T(8,128)}), f32[12,16,128]{2,1,0:T(8,128)S(1)}, u32[]{:S(2)}, u32[]{:S(2)}) async-start(f32[12,16,128]{2,1,0:T(8,128)} %get-tuple-element.14), calls=%async_computation | async-start | bytes 196608 | tf_op jit(solution)/shard_map/all_to_all | solution.py:335
  18.3 16.3 %collective-permute-start.4 = (f32[5,3,16,128]{3,2,1,0:T(8,128)S(1)}, f32[5,3,16,128]{3,2,1,0:T(8,128)}, u32[]{:S(2)}, u32[]{:S(2)}) collective-permute-start(f32[5,3,16,128]{3,2,1,0:T(8,128)S(1)} %get-tuple-element.26), channel_id=1, source_target_pairs={{384,0},{0,384},{385,1},{1,385},{386,2},{2,386},{387,3},{3,387},{3... | collective-permute-start | bytes 368648 | tf_op jit(solution)/shard_map/ppermute | solution.py:360
  19.6 15.7 %collective-permute-start.2 = (f32[5,3,16,128]{3,2,1,0:T(8,128)S(1)}, f32[5,3,16,128]{3,2,1,0:T(8,128)}, u32[]{:S(2)}, u32[]{:S(2)}) collective-permute-start(f32[5,3,16,128]{3,2,1,0:T(8,128)S(1)} %get-tuple-element.27), channel_id=1, source_target_pairs={{378,762},{762,378},{379,763},{763,379},{380,764},{764,380},{381,7... | collective-permute-start | bytes 368648 | tf_op jit(solution)/shard_map/ppermute | solution.py:361
  20.9 29.4 %collective-permute-start.1 = (f32[5,3,16,128]{3,2,1,0:T(8,128)S(1)}, f32[5,3,16,128]{3,2,1,0:T(8,128)S(1)}, u32[]{:S(2)}, u32[]{:S(2)}) collective-permute-start(f32[5,3,16,128]{3,2,1,0:T(8,128)S(1)} %get-tuple-element.26), channel_id=1, source_target_pairs={{6,0},{12,6},{18,12},{24,18},{30,24},{36,30},{42,36},{48,42},{54,4... | collective-permute-start | bytes 368648 | tf_op jit(solution)/shard_map/ppermute | solution.py:359
  32.7 17.6 %collective-permute-start = (f32[5,3,16,128]{3,2,1,0:T(8,128)S(1)}, f32[5,3,16,128]{3,2,1,0:T(8,128)S(1)}, u32[]{:S(2)}, u32[]{:S(2)}) collective-permute-start(f32[5,3,16,128]{3,2,1,0:T(8,128)S(1)} %get-tuple-element.27), channel_id=1, source_target_pairs={{0,6},{6,12},{12,18},{18,24},{24,30},{30,36},{36,42},{42,48},{48,5... | collective-permute-start | bytes 368648 | tf_op jit(solution)/shard_map/ppermute | solution.py:362
  34.6 15.7 %collective-permute-start.5 = (f32[5,3,16,128]{3,2,1,0:T(8,128)}, f32[5,3,16,128]{3,2,1,0:T(8,128)S(1)}, u32[]{:S(2)}, u32[]{:S(2)}) collective-permute-start(f32[5,3,16,128]{3,2,1,0:T(8,128)} %collective-permute-done.4), channel_id=1, source_target_pairs={{0,378},{1,379},{2,380},{3,381},{4,382},{5,383},{384,762},{385,763... | collective-permute-start | bytes 368648 | tf_op jit(solution)/shard_map/ppermute | solution.py:363
  35.3 15.0 %collective-permute-start.3 = (f32[5,3,16,128]{3,2,1,0:T(8,128)}, f32[5,3,16,128]{3,2,1,0:T(8,128)S(1)}, u32[]{:S(2)}, u32[]{:S(2)}) collective-permute-start(f32[5,3,16,128]{3,2,1,0:T(8,128)} %collective-permute-done.2), channel_id=1, source_target_pairs={{378,0},{379,1},{380,2},{381,3},{382,4},{383,5},{762,384},{763,385... | collective-permute-start | bytes 368648 | tf_op jit(solution)/shard_map/ppermute | solution.py:364
  36.7 12.5 %copy-start = (f32[5,8,3,128]{3,1,2,0:T(8,128)S(1)}, f32[5,8,3,128]{3,1,2,0:T(8,128)}, u32[]{:S(2)}) copy-start(f32[5,8,3,128]{3,1,2,0:T(8,128)} %param.6) | copy-start | bytes 184324
  36.7 12.5 %copy-start.1 = (s32[8,16,1]{1,2,0:T(1,128)S(1)}, s32[8,16,1]{1,2,0:T(1,128)}, u32[]{:S(2)}) copy-start(s32[8,16,1]{1,2,0:T(1,128)} %param.7) | copy-start | bytes 1540
  36.7 21.9 %all-to-all-start.1 = ((f32[64,1,128]{2,1,0:T(1,128)}), f32[64,1,128]{2,1,0:T(1,128)S(1)}, u32[]{:S(2)}, u32[]{:S(2)}) async-start(f32[64,1,128]{2,1,0:T(1,128)} %relay.1), calls=%async_computation.1 | async-start | bytes 65536 | tf_op jit(solution)/shard_map/all_to_all | solution.py:345

commit v5 on v4

v5 whole, which is shorter than its diff:
```python
import jax
import jax.numpy as jnp
from jax import lax
from jax.experimental import pallas as pl
from jax.experimental.pallas import tpu as pltpu
from jax.sharding import Mesh
from jax.sharding import PartitionSpec as P

GX = ("gx_0", "gx_1", "gx_2", "gx_3")
PLANE = ("gx_1", "gx_2", "gx_3")
ZLINE = ("gx_0", "gz")

GAMMA = 1.4
EPS_WENO = 1e-06
LAMBDA = (0.1, 0.15, 0.1)
REGISTER_DECAY = -5.0 / 9.0
UPDATE_WEIGHT = 15.0 / 16.0

NV = 5
CX = 8
CY = 16
CZ = 128
ROWS = CX * CY
HALO = 3
SUB = 8
LONG = 16 + 2 * HALO


def primitives(cons):
    inverse = 1.0 / cons[0]
    vels = [cons[k] * inverse for k in (1, 2, 3)]
    kinetic = cons[1] * vels[0] + cons[2] * vels[1] + cons[3] * vels[2]
    pressure = (GAMMA - 1.0) * (cons[4] - 0.5 * kinetic)
    return inverse, vels, pressure


def fetch(pairs, sems):
    copies = [pltpu.make_async_copy(src, dst, sems.at[i]) for i, (src, dst) in enumerate(pairs)]
    for copy in copies:
        copy.start()
    for copy in copies:
        copy.wait()


def line_neighbours():
    n_z, here = lax.axis_size("gz"), lax.axis_index("gz")
    first = lax.axis_index("gx_0") * n_z
    return first + lax.rem(here + n_z - 1, n_z), first + lax.rem(here + 1, n_z)


def open_kernel(
    far_ref, far_top_ref, far_flag_ref, state_ref, out_ref, ends_ref, top_ref, flag_ref, sems
):
    pairs = [(far_ref.at[v], state_ref.at[v]) for v in range(NV)]
    fetch(pairs + [(far_top_ref, top_ref), (far_flag_ref, flag_ref)], sems)
    best = [None] * 3
    for block in range(ROWS // SUB):
        rows = slice(block * SUB, block * SUB + SUB)
        inverse, vels, pressure = primitives([state_ref[v, rows, :] for v in range(NV)])
        sound = jnp.sqrt(GAMMA * pressure * inverse)
        for k in range(3):
            speed = jnp.abs(vels[k]) + sound
            best[k] = speed if block == 0 else jnp.maximum(best[k], speed)
    lane = lax.broadcasted_iota(jnp.int32, (1, CZ), 1)
    packed = jnp.zeros((1, CZ), jnp.float32)
    for k in range(3):
        top = jnp.max(jnp.max(best[k], axis=0, keepdims=True), axis=1, keepdims=True)
        packed = jnp.where(lane == k, top, packed)
    firsts, lasts = [], []
    for v in range(NV):
        turned = state_ref[v].T
        firsts.append(turned[:HALO])
        lasts.append(turned[CZ - HALO :])
    _, after = line_neighbours()
    for to in range(out_ref.shape[0]):
        forward = after == to
        for v in range(NV):
            out_ref[to, v * HALO : v * HALO + HALO, :] = jnp.where(forward, lasts[v], firsts[v])
        out_ref[to, NV * HALO : NV * HALO + 1, :] = packed
    first = plane_place()[0] == 0
    for v in range(NV):
        for i in range(HALO):
            for h in range(CY // SUB):
                low, high = i * CY + h * SUB, (CX - HALO + i) * CY + h * SUB
                ends_ref[v, i, h * SUB : h * SUB + SUB, :] = jnp.where(
                    first, state_ref[v, low : low + SUB, :], state_ref[v, high : high + SUB, :]
                )


def plane_place():
    place, last = 0, 1
    for axis in PLANE:
        place = place * lax.axis_size(axis) + lax.axis_index(axis)
        last = last * lax.axis_size(axis)
    return place, last - 1


def relay_kernel(got_ref, out_ref):
    row = slice(NV * HALO, NV * HALO + 1)
    best = got_ref[0, row, :]
    for i in range(1, got_ref.shape[0]):
        best = jnp.maximum(best, got_ref[i, row, :])
    for to in range(out_ref.shape[0]):
        out_ref[to] = best


def peak_kernel(speed_ref, out_ref):
    best = speed_ref[0]
    for i in range(1, speed_ref.shape[0]):
        best = jnp.maximum(best, speed_ref[i])
    lane = lax.broadcasted_iota(jnp.int32, (1, CZ), 1)
    for k in range(3):
        top = jnp.max(jnp.where(lane == k, best, 0.0), axis=1, keepdims=True)
        out_ref[k] = jnp.broadcast_to(top, (SUB, CZ))


def flux_of(cons, var):
    _, vels, pressure = primitives(cons)
    velocity = vels[var - 1]
    flux = [(cons[v] + pressure if v == 4 else cons[v]) * velocity for v in range(NV)]
    flux[var] = flux[var] + pressure
    return flux


def linear_parts(flux, cons, masks, scale):
    count = len(flux) - 2 * HALO

    def face(j):
        inner, outer = flux[j + 2] + flux[j + 3], flux[j + 1] + flux[j + 4]
        central = 37.0 * inner - 8.0 * outer + (flux[j] + flux[j + 5])
        return central, 7.0 * inner - outer, (cons[j + 4] - cons[j + 1]) - 3.0 * (cons[j + 3] - cons[j + 2])

    faces = [face(j) for j in range(count + 1)]
    base, tilt = [], []
    for low, high, mask in zip(faces, faces[1:], masks):
        base.append(jnp.where(mask, (scale / 12.0) * (high[1] - low[1]), (scale / 60.0) * (high[0] - low[0])))
        tilt.append(jnp.where(mask, (scale / 12.0) * (high[2] - low[2]), 0.0))
    return base, tilt


EPS_SCALED = 4.0 * EPS_WENO
CURVE = 4.0 / 3.0


def bent_faces(flux, cons, alpha):
    count = len(flux) - 2 * HALO + 1
    moved = [alpha * u for u in cons]

    def slopes(vals):
        step = [b - a for a, b in zip(vals, vals[1:])]
        bend = [None] + [b - a for a, b in zip(step, step[1:])]
        turn = [None] + [b - a for a, b in zip(bend[1:], bend[2:])]
        base = [None] + [CURVE * (d * d) + EPS_SCALED for d in bend[1:]]
        return step, bend, turn, base

    def pull(beta_a, beta_b, beta_c, near_turn, far_turn):
        u, w = beta_b / beta_a, beta_b / beta_c
        u, w = u * u, w * w
        w = 3.0 * w
        return ((u + u) * near_turn + w * far_turn) / (6.0 + u + w)

    pe, pd, pt, pk = slopes([f + m for f, m in zip(flux, moved)])
    me, md, mt, mk = slopes([f - m for f, m in zip(flux, moved)])
    out = []
    for j in range(count):
        bc, cd = pe[j + 1], pe[j + 2]
        plus = pull(
            pk[j + 1] + bc * (bc + pd[j + 1]), pk[j + 2] + bc * cd, pk[j + 3] + cd * (cd - pd[j + 3]), pt[j + 1], pt[j + 2]
        )
        bc, cd = me[j + 3], me[j + 2]
        minus = pull(
            mk[j + 4] + bc * (bc - md[j + 4]), mk[j + 3] + bc * cd, mk[j + 2] + cd * (cd + md[j + 2]), mt[j + 3], mt[j + 2]
        )
        out.append(minus - plus)
    return out


def step_kernel(
    speed_ref, state_ref, xlo_ref, xhi_ref, seam_ref, helped_ref, got_ref, top_ref, flag_ref, old_reg_ref,
    far_state_ref, far_reg_ref,
    xmask_ref, ymask_ref, xf_ref, yf_ref, yu_ref, zf_ref, zu_ref, line, side_f, side_u, acc_y, acc_z,
    reg_ref, state_out, reg_out, sems,
):
    def load(v):
        return pltpu.make_async_copy(old_reg_ref.at[v], reg_ref.at[v], sems.at[2, v])

    for v in range(NV):
        load(v).start()

    square = (CY, CY)
    diagonal = lax.broadcasted_iota(jnp.int32, square, 0) == lax.broadcasted_iota(jnp.int32, square, 1)
    for x in range(CX):
        spread = jnp.broadcast_to(flag_ref[x].astype(jnp.float32), square)
        column = jnp.max(jnp.where(diagonal, spread, 0.0), axis=1, keepdims=True)
        xmask_ref[x * CY : x * CY + CY, :] = jnp.broadcast_to(column, (CY, CZ)) * (LAMBDA[0] / 12.0)
    for y in range(CY):
        ymask_ref[y] = xmask_ref[pl.ds(y, CX, stride=CY), :] * (LAMBDA[1] / LAMBDA[0])
    zmask = xmask_ref[...].T[:SUB] * (LAMBDA[2] / LAMBDA[0])

    before, after = line_neighbours()
    for v in range(NV):
        rows = slice(v * HALO, v * HALO + HALO)
        line[v, :HALO, :] = got_ref[before, rows, :]
        line[v, HALO : HALO + CZ, :] = state_ref[v].T
        line[v, HALO + CZ : 2 * HALO + CZ, :] = got_ref[after, rows, :]

    def keep(to, cons, var, flux_ref, cons_ref):
        flux = flux_of(cons, var)
        for v in range(NV):
            flux_ref[v, to] = flux[v]
            cons_ref[v, to] = cons[v]

    for i in range(LONG):
        keep(i, [line[v, pl.ds(i, SUB, stride=CZ // SUB), :] for v in range(NV)], 3, zf_ref, zu_ref)
    for i in range(CY):
        cons = [state_ref[v, pl.ds(i, CX, stride=CY), :] for v in range(NV)]
        keep(i + HALO, cons, 2, yf_ref, yu_ref)
        if i < HALO:
            keep(HALO - 1 - i, [-c if v == 2 else c for v, c in enumerate(cons)], 2, yf_ref, yu_ref)
            keep(HALO + CY + i, [top_ref[v, i] for v in range(NV)], 2, yf_ref, yu_ref)

    alphas = [speed_ref[k] for k in range(3)]
    halves = [slice(h * SUB, h * SUB + SUB) for h in range(CY // SUB)]

    place, last = plane_place()
    for i in range(HALO):
        for rows in halves:
            for at, side_ref, end in ((i, xlo_ref, 0), (HALO + i, xhi_ref, last)):
                cons = [
                    jnp.where(
                        place == end, seam_ref[v, i, rows, :] + helped_ref[v, i, rows, :], side_ref[v, i, rows, :]
                    )
                    for v in range(NV)
                ]
                flux = flux_of(cons, 1)
                for v in range(NV):
                    side_f[v, at, rows, :] = flux[v]
                    side_u[v, at, rows, :] = cons[v]

    for block in range(ROWS // SUB):
        rows = slice(block * SUB, block * SUB + SUB)
        flux = flux_of([state_ref[v, rows, :] for v in range(NV)], 1)
        for v in range(NV):
            xf_ref[v, rows, :] = flux[v]

    def copies(v):
        return [
            pltpu.make_async_copy(state_out.at[v], far_state_ref.at[v], sems.at[0, v]),
            pltpu.make_async_copy(reg_out.at[v], far_reg_ref.at[v], sems.at[1, v]),
        ]

    def per_var(v, carry):
        flux, cons = [zf_ref[v, i] for i in range(LONG)], [zu_ref[v, i] for i in range(LONG)]
        bent = bent_faces(flux, cons, alphas[2])
        base, tilt = linear_parts(flux, cons, [zmask > 0.0] * CY, LAMBDA[2])
        for i in range(CY):
            acc_z[pl.ds(i, SUB, stride=CZ // SUB), :] = (
                base[i] + alphas[2] * tilt[i] + zmask * (bent[i + 1] - bent[i])
            )
        flux, cons = [yf_ref[v, i] for i in range(LONG)], [yu_ref[v, i] for i in range(LONG)]
        bent = bent_faces(flux, cons, alphas[1])
        base, tilt = linear_parts(flux, cons, [ymask_ref[i] > 0.0 for i in range(CY)], LAMBDA[1])
        for i in range(CY):
            acc_y[pl.ds(i, CX, stride=CY), :] = (
                base[i] + alphas[1] * tilt[i] + ymask_ref[i] * (bent[i + 1] - bent[i])
            )
        spread = acc_z[...].T
        load(v).wait()
        for rows in halves:
            at = [slice(i * CY + rows.start, i * CY + rows.stop) for i in range(CX)]
            flux = (
                [side_f[v, i, rows, :] for i in range(HALO)]
                + [xf_ref[v, here, :] for here in at]
                + [side_f[v, HALO + i, rows, :] for i in range(HALO)]
            )
            cons = (
                [side_u[v, i, rows, :] for i in range(HALO)]
                + [state_ref[v, here, :] for here in at]
                + [side_u[v, HALO + i, rows, :] for i in range(HALO)]
            )
            bent = bent_faces(flux, cons, alphas[0])
            base, tilt = linear_parts(flux, cons, [xmask_ref[here, :] > 0.0 for here in at], LAMBDA[0])
            for i, here in enumerate(at):
                x_part = base[i] + alphas[0] * tilt[i] + xmask_ref[here, :] * (bent[i + 1] - bent[i])
                change = x_part + acc_y[here, :] + spread[here]
                register = REGISTER_DECAY * reg_ref[v, here, :] - change
                reg_out[v, here, :] = register
                state_out[v, here, :] = state_ref[v, here, :] + UPDATE_WEIGHT * register
        for copy in copies(v):
            copy.start()
        return carry

    lax.fori_loop(0, NV, per_var, 0)
    for v in range(NV):
        for copy in copies(v):
            copy.wait()


def f32(*shape):
    return jax.ShapeDtypeStruct(shape, jnp.float32)


def near(*shape):
    return pltpu.VMEM(shape, jnp.float32)


ROOM = pltpu.CompilerParams(vmem_limit_bytes=16 * 1024 * 1024)


def held(value):
    return pltpu.with_memory_space_constraint(value, pltpu.VMEM)


def afar(value):
    return pltpu.with_memory_space_constraint(value, pltpu.HBM)


def advance(state, register, top_ghost, flags):
    flat = state.reshape(NV, ROWS, CZ)
    halves, n_z = lax.axis_size("gx_0"), lax.axis_size("gz")
    n_plane = lax.axis_size("gx_1") * lax.axis_size("gx_2") * lax.axis_size("gx_3")

    far = pl.BlockSpec(memory_space=pltpu.HBM)
    close = pl.BlockSpec(memory_space=pltpu.VMEM)
    planes = (NV, LONG, SUB, CZ)
    near_state, own, ends, top, flag = pl.pallas_call(
        open_kernel,
        in_specs=[far] * 3,
        out_shape=(
            near(NV, ROWS, CZ), near(halves * n_z, NV * HALO + 1, CZ), near(NV, HALO, CY, CZ),
            near(NV, HALO, CX, CZ), pltpu.VMEM((CX, 1, CY), jnp.int32),
        ),
        scratch_shapes=[pltpu.SemaphoreType.DMA((NV + 2,))],
        compiler_params=ROOM, name="open",
    )(afar(flat), afar(top_ghost.transpose(0, 2, 1, 3)), afar(flags.transpose(0, 2, 1)))
    by_line = lax.all_to_all(held(own), ZLINE, 0, 0, tiled=True)
    relayed = pl.pallas_call(relay_kernel, out_shape=near(n_plane, 1, CZ), compiler_params=ROOM, name="relay")(held(by_line))
    speeds = lax.all_to_all(held(relayed), PLANE, 0, 0, tiled=True)
    ahead = [(i, i + 1) for i in range(n_plane - 1)]
    last = n_plane - 1

    def at(half, place, z):
        return (half * n_plane + place) * n_z + z

    soon = 3 if n_plane > 8 and n_z > 4 else 0
    seams, handed, passed = [], [], []
    for z in range(n_z):
        seams += [(at(1, 0, z), at(0, last, z)), (at(1, last, z), at(0, 0, z))]
        ends_of = ((0, last, 1 + z), (last, 0, last - 1 - z))
        for own_end, far_end, helper in ends_of:
            if z < soon:
                handed.append((at(0, own_end, z), at(0, helper, n_z - 1)))
                passed.append((at(0, helper, n_z - 1), at(1, far_end, z)))
            else:
                seams.append((at(0, own_end, z), at(1, far_end, z)))

    blocks = near_state.reshape(state.shape)
    upper, lower = blocks[:, CX - HALO :], blocks[:, :HALO]
    seam = lax.ppermute(ends, GX + ("gz",), seams)
    helped = lax.ppermute(ends, GX + ("gz",), handed)
    helped = lax.ppermute(helped, GX + ("gz",), passed)
    xhi = lax.ppermute(lower, PLANE, [(b, a) for a, b in ahead])
    xlo = lax.ppermute(upper, PLANE, ahead)

    peaks = pl.pallas_call(peak_kernel, out_shape=near(3, SUB, CZ), compiler_params=ROOM, name="peak")(held(speeds))

    new_state, new_register = pl.pallas_call(
        step_kernel,
        out_shape=(f32(NV, ROWS, CZ), f32(NV, ROWS, CZ)),
        in_specs=[close] * 9 + [far],
        out_specs=(far, far),
        scratch_shapes=[
            pltpu.VMEM(shape, jnp.float32)
            for shape in (
                (ROWS, CZ), (CY, CX, CZ), (NV, ROWS, CZ), planes, planes, planes, planes, (NV, CZ + 8, ROWS),
                (NV, 2 * HALO, CY, CZ), (NV, 2 * HALO, CY, CZ), (ROWS, CZ), (CZ, ROWS),
                (NV, ROWS, CZ), (NV, ROWS, CZ), (NV, ROWS, CZ),
            )
        ]
        + [
            pltpu.SemaphoreType.DMA((3, NV)),
        ],
        compiler_params=ROOM, name="step",
    )(
        *map(held, (peaks, near_state, xlo, xhi, seam, helped, by_line, top, flag)),
        afar(register.reshape(NV, ROWS, CZ)),
    )
    return (new_state.reshape(state.shape), new_register.reshape(state.shape))


def solution(mesh):
    finer = Mesh(
        mesh.devices.reshape(2, 8, 4, 2, mesh.shape["gz"]), ("gx_0", "gx_1", "gx_2", "gx_3", "gz")
    )
    placed = P(None, GX, None, "gz")
    return jax.shard_map(
        advance,
        mesh=finer,
        in_specs=(placed, placed, placed, P(GX, None, "gz")),
        out_specs=(placed, placed),
        check_vma=False,
    )
```

time: 63.8 us -> 63 us (0.987)
  blocking collectives: 0 us -> 19.8 us
  starting transfers between devices: 45.9 us -> 35.1 us
  waiting for transfers between devices: 8.19 us -> 0.02 us
  Pallas kernels: 8.42 us -> 6.96 us
    all_to_all x0 -> x1, blocking collectives: none -> 19.8 us  [advance(): speeds = lax.all_to_all(held(relayed), PLANE, 0, 0, tiled=True)]
    all_to_all x1 -> x0, starting transfers between devices: 12.5 us -> none  [advance(): speeds = lax.all_to_all(held(relayed), PLANE, 0, 0, tiled=True)]
    all_to_all x1 -> x0, waiting for transfers between devices: 8.18 us -> none  [advance(): speeds = lax.all_to_all(held(relayed), PLANE, 0, 0, tiled=True)]
    ppermute x1, starting transfers between devices: 11.8 us -> 15.5 us  [advance(): xhi = lax.ppermute(lower, PLANE, [(b, a) for a, b in ahead])]
    ppermute x4 -> x3, starting transfers between devices: 3.96 us -> 2.01 us  [the longest x1 0.67 us: advance(): helped = lax.ppermute(ends, GX + ('gz',), handed)]
    pallas_call x3 -> x2, Pallas kernels: 3 us -> 2.11 us  [the longest x1 1.96 us: advance(): pl.pallas_call(open_kernel, in_specs=[far] * 3, out_shape=(near(NV, ROWS,...]
  transfers between devices with their start and end apart: 8 -> 6, of which waited for: 1 -> 0; matrix products, arithmetic and copies ran while one was open for 0% -> 0% of each run, Pallas kernels for 3% -> 0%
where the time goes in v5:
time: 63 us; the launch traced here: 62.6 us
  starting transfers between devices  35.1 us (56%)
  blocking collectives  19.8 us (31%)
  Pallas kernels  6.96 us (11%)
  between operations  0.73 us (1%)
    all_to_all x1, blocking collectives, advance(): speeds = lax.all_to_all(held(relayed), PLANE, 0, 0, tiled=True)  19.8 us
    all_to_all x1, starting transfers between devices, advance(): by_line = lax.all_to_all(held(own), ZLINE, 0, 0, tiled=True)  15.7 us
    ppermute x1, starting transfers between devices, advance(): xhi = lax.ppermute(lower, PLANE, [(b, a) for a, b in ahead])  15.5 us
    pallas_call x1, Pallas kernels, advance(): pl.pallas_call(step_kernel, out_shape=(f32(NV, ROWS, CZ), f32(NV, ROWS, C...  4.81 us
    pallas_call x1, Pallas kernels, advance(): pl.pallas_call(open_kernel, in_specs=[far] * 3, out_shape=(near(NV, ROWS,...  1.96 us
    ppermute x1, starting transfers between devices, advance(): xlo = lax.ppermute(upper, PLANE, ahead)  1.92 us
  transfers between devices with their start and end apart: 6, of which 0 were waited for; matrix products, arithmetic and copies ran while one was open for 0% of the time, Pallas kernels for 0%

profile of v5, /device:TPU:1, one launch (start us, length us, event | category | flops | bytes accessed | tf_op | source)
XLA Modules:
  0.0 62.6 jit_solution(15189249136978623087)
XLA Ops:
  0.6 2.0 %open.1 = (f32[5,128,128]{2,1,0:T(8,128)S(1)}, f32[12,16,128]{2,1,0:T(8,128)}, f32[5,3,16,128]{3,2,1,0:T(8,128)S(1)}, f32[5,3,8,128]{3,2,1,0:T(8,128)S(1)}, s32[8,1,16]{2,1,0:T(1,128)S(1)}) custom-call(f32[5,128,128]{2,1,0:T(8,128)} %bitcast.11, f32[5,3,8,128]{3,2,1,0:T(8,128)} %bitcast.12, s32[8,1,16]{2,1,0:T(1,128)} %bitcast.13), custom_call_target="tpu_custom_call" | custom-call | tf_op jit(solution)/shard_map/open/pallas_call | solution.py:326
  2.6 0.7 %collective-permute-start.3 = (f32[5,3,16,128]{3,2,1,0:T(8,128)S(1)}, f32[5,3,16,128]{3,2,1,0:T(8,128)S(1)}, u32[]{:S(2)}, u32[]{:S(2)}) collective-permute-start(f32[5,3,16,128]{3,2,1,0:T(8,128)S(1)} %get-tuple-element.11), channel_id=1, source_target_pairs={{0,11},{378,377},{1,17},{379,371},{2,23},{380,365}} | collective-permute-start | bytes 368648 | tf_op jit(solution)/shard_map/ppermute | solution.py:360
  3.3 0.7 %collective-permute-start.2 = (f32[5,3,16,128]{3,2,1,0:T(8,128)S(1)}, f32[5,3,16,128]{3,2,1,0:T(8,128)S(1)}, u32[]{:S(2)}, u32[]{:S(2)}) collective-permute-start(f32[5,3,16,128]{3,2,1,0:T(8,128)S(1)} %get-tuple-element.11), channel_id=1, source_target_pairs={{384,378},{762,0},{385,379},{763,1},{386,380},{764,2},{387,381},{7... | collective-permute-start | bytes 368648 | tf_op jit(solution)/shard_map/ppermute | solution.py:359
  4.0 15.7 %all-to-all-start = ((f32[12,16,128]{2,1,0:T(8,128)}), f32[12,16,128]{2,1,0:T(8,128)S(1)}, u32[]{:S(2)}, u32[]{:S(2)}) async-start(f32[12,16,128]{2,1,0:T(8,128)} %get-tuple-element.9), calls=%async_computation | async-start | bytes 196608 | tf_op jit(solution)/shard_map/all_to_all | solution.py:336
  19.7 15.5 %collective-permute-start.1 = (f32[5,3,16,128]{3,2,1,0:T(8,128)S(1)}, f32[5,3,16,128]{3,2,1,0:T(8,128)S(1)}, u32[]{:S(2)}, u32[]{:S(2)}) collective-permute-start(f32[5,3,16,128]{3,2,1,0:T(8,128)S(1)} %get-tuple-element.16), channel_id=1, source_target_pairs={{6,0},{12,6},{18,12},{24,18},{30,24},{36,30},{42,36},{48,42},{54,4... | collective-permute-start | bytes 368648 | tf_op jit(solution)/shard_map/ppermute | solution.py:362
  35.2 1.9 %collective-permute-start = (f32[5,3,16,128]{3,2,1,0:T(8,128)S(1)}, f32[5,3,16,128]{3,2,1,0:T(8,128)S(1)}, u32[]{:S(2)}, u32[]{:S(2)}) collective-permute-start(f32[5,3,16,128]{3,2,1,0:T(8,128)S(1)} %get-tuple-element.17), channel_id=1, source_target_pairs={{0,6},{6,12},{12,18},{18,24},{24,30},{30,36},{36,42},{42,48},{48,5... | collective-permute-start | bytes 368648 | tf_op jit(solution)/shard_map/ppermute | solution.py:363
  37.1 0.0 collective-permute-done.3
  37.1 0.7 %collective-permute-start.4 = (f32[5,3,16,128]{3,2,1,0:T(8,128)S(1)}, f32[5,3,16,128]{3,2,1,0:T(8,128)S(1)}, u32[]{:S(2)}, u32[]{:S(2)}) collective-permute-start(f32[5,3,16,128]{3,2,1,0:T(8,128)S(1)} %collective-permute-done.3), channel_id=1, source_target_pairs={{11,762},{377,384},{17,763},{371,385},{23,764},{365,386}} | collective-permute-start | bytes 368648 | tf_op jit(solution)/shard_map/ppermute | solution.py:361
  37.8 0.0 all-to-all-done.got_ref
  37.8 19.8 %all_to_all.10.speed_ref = f32[64,1,128]{2,1,0:T(1,128)S(1)} all-to-all(f32[64,1,128]{2,1,0:T(1,128)S(1)} %relay.1), channel_id=1, replica_groups=mesh['gx_0'=2,'gx_1'=8,'gx_2'=4,'gx_3'=2,'gz'=6] {'gx_1','gx_2','gx_3'}, dimensions={0} | all-to-all | bytes 65536 | tf_op jit(solution)/shard_map/all_to_all | solution.py:338
  57.6 0.1 peak.1.speed_ref
  57.8 0.0 collective-permute-done.2.seam_ref
  57.8 0.0 collective-permute-done.1.xhi_ref
  57.8 0.0 collective-permute-done.xlo_ref
  57.8 0.0 collective-permute-done.4.helped_ref
  57.8 4.8 %step.1 = (f32[5,128,128]{2,1,0:T(8,128)}, f32[5,128,128]{2,1,0:T(8,128)}) custom-call(f32[3,8,128]{2,1,0:T(8,128)S(1)} %peak.1.speed_ref, f32[5,128,128]{2,1,0:T(8,128)S(1)} %get-tuple-element.10.state_ref, f32[5,3,16,128]{3,2,1,0:T(8,128)S(1)} %collective-permute-done.xlo_ref, f32[5,3,16,128]{3,2,1,0:T(8,128)S(1)} %collective-permute-done.1.xhi_ref, ...), custom_call_target="tpu_custom_call" | custom-call | tf_op jit(solution)/shard_map/step/pallas_call | solution.py:367
  (2 shorter events, 0.0 us)
Async XLA Ops:
  2.6 34.5 %collective-permute-start.3 = (f32[5,3,16,128]{3,2,1,0:T(8,128)S(1)}, f32[5,3,16,128]{3,2,1,0:T(8,128)S(1)}, u32[]{:S(2)}, u32[]{:S(2)}) collective-permute-start(f32[5,3,16,128]{3,2,1,0:T(8,128)S(1)} %get-tuple-element.11), channel_id=1, source_target_pairs={{0,11},{378,377},{1,17},{379,371},{2,23},{380,365}} | collective-permute-start | bytes 368648 | tf_op jit(solution)/shard_map/ppermute | solution.py:360
  3.3 54.5 %collective-permute-start.2 = (f32[5,3,16,128]{3,2,1,0:T(8,128)S(1)}, f32[5,3,16,128]{3,2,1,0:T(8,128)S(1)}, u32[]{:S(2)}, u32[]{:S(2)}) collective-permute-start(f32[5,3,16,128]{3,2,1,0:T(8,128)S(1)} %get-tuple-element.11), channel_id=1, source_target_pairs={{384,378},{762,0},{385,379},{763,1},{386,380},{764,2},{387,381},{7... | collective-permute-start | bytes 368648 | tf_op jit(solution)/shard_map/ppermute | solution.py:359
  4.0 33.8 %all-to-all-start = ((f32[12,16,128]{2,1,0:T(8,128)}), f32[12,16,128]{2,1,0:T(8,128)S(1)}, u32[]{:S(2)}, u32[]{:S(2)}) async-start(f32[12,16,128]{2,1,0:T(8,128)} %get-tuple-element.9), calls=%async_computation | async-start | bytes 196608 | tf_op jit(solution)/shard_map/all_to_all | solution.py:336
  19.7 38.1 %collective-permute-start.1 = (f32[5,3,16,128]{3,2,1,0:T(8,128)S(1)}, f32[5,3,16,128]{3,2,1,0:T(8,128)S(1)}, u32[]{:S(2)}, u32[]{:S(2)}) collective-permute-start(f32[5,3,16,128]{3,2,1,0:T(8,128)S(1)} %get-tuple-element.16), channel_id=1, source_target_pairs={{6,0},{12,6},{18,12},{24,18},{30,24},{36,30},{42,36},{48,42},{54,4... | collective-permute-start | bytes 368648 | tf_op jit(solution)/shard_map/ppermute | solution.py:362
  35.2 22.6 %collective-permute-start = (f32[5,3,16,128]{3,2,1,0:T(8,128)S(1)}, f32[5,3,16,128]{3,2,1,0:T(8,128)S(1)}, u32[]{:S(2)}, u32[]{:S(2)}) collective-permute-start(f32[5,3,16,128]{3,2,1,0:T(8,128)S(1)} %get-tuple-element.17), channel_id=1, source_target_pairs={{0,6},{6,12},{12,18},{18,24},{24,30},{30,36},{36,42},{42,48},{48,5... | collective-permute-start | bytes 368648 | tf_op jit(solution)/shard_map/ppermute | solution.py:363
  37.1 20.7 %collective-permute-start.4 = (f32[5,3,16,128]{3,2,1,0:T(8,128)S(1)}, f32[5,3,16,128]{3,2,1,0:T(8,128)S(1)}, u32[]{:S(2)}, u32[]{:S(2)}) collective-permute-start(f32[5,3,16,128]{3,2,1,0:T(8,128)S(1)} %collective-permute-done.3), channel_id=1, source_target_pairs={{11,762},{377,384},{17,763},{371,385},{23,764},{365,386}} | collective-permute-start | bytes 368648 | tf_op jit(solution)/shard_map/ppermute | solution.py:361

commit v6 on v5

--- a/solution.py
+++ b/solution.py
@@ -175,24 +175,52 @@
     return out
 
 
-def step_kernel(
-    speed_ref, state_ref, xlo_ref, xhi_ref, seam_ref, helped_ref, got_ref, top_ref, flag_ref, old_reg_ref,
-    far_state_ref, far_reg_ref,
-    xmask_ref, ymask_ref, xf_ref, yf_ref, yu_ref, zf_ref, zu_ref, line, side_f, side_u, acc_y, acc_z,
-    reg_ref, state_out, reg_out, sems,
-):
-    def load(v):
-        return pltpu.make_async_copy(old_reg_ref.at[v], reg_ref.at[v], sems.at[2, v])
-
-    for v in range(NV):
-        load(v).start()
-
+def prepare_kernel(state_ref, top_ref, flag_ref, xmask_ref, yf_ref, yu_ref, ybase_ref, ytilt_ref):
     square = (CY, CY)
     diagonal = lax.broadcasted_iota(jnp.int32, square, 0) == lax.broadcasted_iota(jnp.int32, square, 1)
     for x in range(CX):
         spread = jnp.broadcast_to(flag_ref[x].astype(jnp.float32), square)
         column = jnp.max(jnp.where(diagonal, spread, 0.0), axis=1, keepdims=True)
         xmask_ref[x * CY : x * CY + CY, :] = jnp.broadcast_to(column, (CY, CZ)) * (LAMBDA[0] / 12.0)
+
+    def keep(to, cons, var, flux_ref, cons_ref):
+        flux = flux_of(cons, var)
+        for v in range(NV):
+            flux_ref[v, to] = flux[v]
+            cons_ref[v, to] = cons[v]
+
+    for i in range(CY):
+        cons = [state_ref[v, pl.ds(i, CX, stride=CY), :] for v in range(NV)]
+        keep(i + HALO, cons, 2, yf_ref, yu_ref)
+        if i < HALO:
+            keep(HALO - 1 - i, [-c if v == 2 else c for v, c in enumerate(cons)], 2, yf_ref, yu_ref)
+            keep(HALO + CY + i, [top_ref[v, i] for v in range(NV)], 2, yf_ref, yu_ref)
+    masks = [xmask_ref[pl.ds(i, CX, stride=CY), :] > 0.0 for i in range(CY)]
+
+    def per_var(v, carry):
+        planes = range(LONG)
+        base, tilt = linear_parts([yf_ref[v, i] for i in planes], [yu_ref[v, i] for i in planes], masks, LAMBDA[1])
+        for i in range(CY):
+            ybase_ref[v, i] = base[i]
+            ytilt_ref[v, i] = tilt[i]
+        return carry
+
+    lax.fori_loop(0, NV, per_var, 0)
+
+
+def step_kernel(
+    speed_ref, state_ref, xlo_ref, xhi_ref, seam_ref, helped_ref, got_ref,
+    xmask_ref, yf_ref, yu_ref, ybase_ref, ytilt_ref, old_reg_ref,
+    far_state_ref, far_reg_ref,
+    ymask_ref, xf_ref, zf_ref, zu_ref, line, side_f, side_u, acc_y, acc_z,
+    reg_ref, state_out, reg_out, sems,
+):
+    def load(v):
+        return pltpu.make_async_copy(old_reg_ref.at[v], reg_ref.at[v], sems.at[2, v])
+
+    for v in range(NV):
+        load(v).start()
+
     for y in range(CY):
         ymask_ref[y] = xmask_ref[pl.ds(y, CX, stride=CY), :] * (LAMBDA[1] / LAMBDA[0])
     zmask = xmask_ref[...].T[:SUB] * (LAMBDA[2] / LAMBDA[0])
@@ -212,12 +240,7 @@
 
     for i in range(LONG):
         keep(i, [line[v, pl.ds(i, SUB, stride=CZ // SUB), :] for v in range(NV)], 3, zf_ref, zu_ref)
-    for i in range(CY):
-        cons = [state_ref[v, pl.ds(i, CX, stride=CY), :] for v in range(NV)]
-        keep(i + HALO, cons, 2, yf_ref, yu_ref)
-        if i < HALO:
-            keep(HALO - 1 - i, [-c if v == 2 else c for v, c in enumerate(cons)], 2, yf_ref, yu_ref)
-            keep(HALO + CY + i, [top_ref[v, i] for v in range(NV)], 2, yf_ref, yu_ref)
+
 
     alphas = [speed_ref[k] for k in range(3)]
     halves = [slice(h * SUB, h * SUB + SUB) for h in range(CY // SUB)]
@@ -259,10 +282,9 @@
             )
         flux, cons = [yf_ref[v, i] for i in range(LONG)], [yu_ref[v, i] for i in range(LONG)]
         bent = bent_faces(flux, cons, alphas[1])
-        base, tilt = linear_parts(flux, cons, [ymask_ref[i] > 0.0 for i in range(CY)], LAMBDA[1])
         for i in range(CY):
             acc_y[pl.ds(i, CX, stride=CY), :] = (
-                base[i] + alphas[1] * tilt[i] + ymask_ref[i] * (bent[i + 1] - bent[i])
+                ybase_ref[v, i] + alphas[1] * ytilt_ref[v, i] + ymask_ref[i] * (bent[i + 1] - bent[i])
             )
         spread = acc_z[...].T
         load(v).wait()
@@ -334,6 +356,12 @@
         compiler_params=ROOM, name="open",
     )(afar(flat), afar(top_ghost.transpose(0, 2, 1, 3)), afar(flags.transpose(0, 2, 1)))
     by_line = lax.all_to_all(held(own), ZLINE, 0, 0, tiled=True)
+    strips = (NV, CY, SUB, CZ)
+    xmask, yf, yu, ybase, ytilt = pl.pallas_call(
+        prepare_kernel,
+        out_shape=(near(ROWS, CZ), near(*planes), near(*planes), near(*strips), near(*strips)),
+        compiler_params=ROOM, name="prepare",
+    )(held(near_state), held(top), held(flag))
     relayed = pl.pallas_call(relay_kernel, out_shape=near(n_plane, 1, CZ), compiler_params=ROOM, name="relay")(held(by_line))
     speeds = lax.all_to_all(held(relayed), PLANE, 0, 0, tiled=True)
     ahead = [(i, i + 1) for i in range(n_plane - 1)]
@@ -367,12 +395,12 @@
     new_state, new_register = pl.pallas_call(
         step_kernel,
         out_shape=(f32(NV, ROWS, CZ), f32(NV, ROWS, CZ)),
-        in_specs=[close] * 9 + [far],
+        in_specs=[close] * 12 + [far],
         out_specs=(far, far),
         scratch_shapes=[
             pltpu.VMEM(shape, jnp.float32)
             for shape in (
-                (ROWS, CZ), (CY, CX, CZ), (NV, ROWS, CZ), planes, planes, planes, planes, (NV, CZ + 8, ROWS),
+                (CY, CX, CZ), (NV, ROWS, CZ), planes, planes, (NV, CZ + 8, ROWS),
                 (NV, 2 * HALO, CY, CZ), (NV, 2 * HALO, CY, CZ), (ROWS, CZ), (CZ, ROWS),
                 (NV, ROWS, CZ), (NV, ROWS, CZ), (NV, ROWS, CZ),
             )
@@ -382,7 +410,7 @@
         ],
         compiler_params=ROOM, name="step",
     )(
-        *map(held, (peaks, near_state, xlo, xhi, seam, helped, by_line, top, flag)),
+        *map(held, (peaks, near_state, xlo, xhi, seam, helped, by_line, xmask, yf, yu, ybase, ytilt)),
         afar(register.reshape(NV, ROWS, CZ)),
     )
     return (new_state.reshape(state.shape), new_register.reshape(state.shape))

time: 63 us -> 64.1 us (1.017)
  blocking collectives: 19.8 us -> 0 us
  starting transfers between devices: 35.1 us -> 46.2 us
  waiting for transfers between devices: 0.02 us -> 9.01 us
  Pallas kernels: 6.96 us -> 7.7 us
    all_to_all x1 -> x0, blocking collectives: 19.8 us -> none  [advance(): speeds = lax.all_to_all(held(relayed), PLANE, 0, 0, tiled=True)]
    all_to_all x0 -> x1, starting transfers between devices: none -> 11.1 us  [advance(): speeds = lax.all_to_all(held(relayed), PLANE, 0, 0, tiled=True)]
    all_to_all x0 -> x1, waiting for transfers between devices: none -> 9 us  [advance(): speeds = lax.all_to_all(held(relayed), PLANE, 0, 0, tiled=True)]
  transfers between devices with their start and end apart: 6 -> 7, of which waited for: 0 -> 1; matrix products, arithmetic and copies ran while one was open for 0% -> 0% of each run, Pallas kernels for 0% -> 2%
where the time goes in v6:
time: 64.1 us; the launch traced here: 63.7 us
  starting transfers between devices  46.2 us (72%)
  waiting for transfers between devices  9.01 us (14%)
  Pallas kernels  7.7 us (12%)
  between operations  0.74 us (1%)
    all_to_all x1, starting transfers between devices, advance(): by_line = lax.all_to_all(held(own), ZLINE, 0, 0, tiled=True)  15.7 us
    ppermute x1, starting transfers between devices, advance(): xhi = lax.ppermute(lower, PLANE, [(b, a) for a, b in ahead])  15.5 us
    all_to_all x1, starting transfers between devices, advance(): speeds = lax.all_to_all(held(relayed), PLANE, 0, 0, tiled=True)  11.1 us
    all_to_all x1, waiting for transfers between devices, advance(): speeds = lax.all_to_all(held(relayed), PLANE, 0, 0, tiled=True)  9 us
    pallas_call x1, Pallas kernels, advance(): pl.pallas_call(step_kernel, out_shape=(f32(NV, ROWS, CZ), f32(NV, ROWS, C...  4.51 us
    pallas_call x1, Pallas kernels, advance(): pl.pallas_call(open_kernel, in_specs=[far] * 3, out_shape=(near(NV, ROWS,...  1.96 us
    ppermute x1, starting transfers between devices, advance(): xlo = lax.ppermute(upper, PLANE, ahead)  1.92 us
  transfers between devices with their start and end apart: 7, of which 1 were waited for; matrix products, arithmetic and copies ran while one was open for 0% of the time, Pallas kernels for 2%

profile of v6, /device:TPU:1, one launch (start us, length us, event | category | flops | bytes accessed | tf_op | source)
XLA Modules:
  0.0 63.7 jit_solution(8092432380863911024)
XLA Ops:
  0.6 2.0 %open.1 = (f32[5,128,128]{2,1,0:T(8,128)S(1)}, f32[12,16,128]{2,1,0:T(8,128)}, f32[5,3,16,128]{3,2,1,0:T(8,128)S(1)}, f32[5,3,8,128]{3,2,1,0:T(8,128)S(1)}, s32[8,1,16]{2,1,0:T(1,128)S(1)}) custom-call(f32[5,128,128]{2,1,0:T(8,128)} %bitcast.10, f32[5,3,8,128]{3,2,1,0:T(8,128)} %bitcast.12, s32[8,1,16]{2,1,0:T(1,128)} %bitcast.13), custom_call_target="tpu_custom_call" | custom-call | tf_op jit(solution)/shard_map/open/pallas_call | solution.py:348
  2.6 0.7 %collective-permute-start.3 = (f32[5,3,16,128]{3,2,1,0:T(8,128)S(1)}, f32[5,3,16,128]{3,2,1,0:T(8,128)S(1)}, u32[]{:S(2)}, u32[]{:S(2)}) collective-permute-start(f32[5,3,16,128]{3,2,1,0:T(8,128)S(1)} %get-tuple-element.16), channel_id=1, source_target_pairs={{0,11},{378,377},{1,17},{379,371},{2,23},{380,365}} | collective-permute-start | bytes 368648 | tf_op jit(solution)/shard_map/ppermute | solution.py:388
  3.3 0.7 %collective-permute-start.2 = (f32[5,3,16,128]{3,2,1,0:T(8,128)S(1)}, f32[5,3,16,128]{3,2,1,0:T(8,128)S(1)}, u32[]{:S(2)}, u32[]{:S(2)}) collective-permute-start(f32[5,3,16,128]{3,2,1,0:T(8,128)S(1)} %get-tuple-element.16), channel_id=1, source_target_pairs={{384,378},{762,0},{385,379},{763,1},{386,380},{764,2},{387,381},{7... | collective-permute-start | bytes 368648 | tf_op jit(solution)/shard_map/ppermute | solution.py:387
  4.0 15.7 %all-to-all-start = ((f32[12,16,128]{2,1,0:T(8,128)}), f32[12,16,128]{2,1,0:T(8,128)S(1)}, u32[]{:S(2)}, u32[]{:S(2)}) async-start(f32[12,16,128]{2,1,0:T(8,128)} %get-tuple-element.14), calls=%async_computation | async-start | bytes 196608 | tf_op jit(solution)/shard_map/all_to_all | solution.py:358
  19.7 15.5 %collective-permute-start.1 = (f32[5,3,16,128]{3,2,1,0:T(8,128)S(1)}, f32[5,3,16,128]{3,2,1,0:T(8,128)S(1)}, u32[]{:S(2)}, u32[]{:S(2)}) collective-permute-start(f32[5,3,16,128]{3,2,1,0:T(8,128)S(1)} %get-tuple-element.26), channel_id=1, source_target_pairs={{6,0},{12,6},{18,12},{24,18},{30,24},{36,30},{42,36},{48,42},{54,4... | collective-permute-start | bytes 368648 | tf_op jit(solution)/shard_map/ppermute | solution.py:390
  35.2 1.9 %collective-permute-start = (f32[5,3,16,128]{3,2,1,0:T(8,128)S(1)}, f32[5,3,16,128]{3,2,1,0:T(8,128)S(1)}, u32[]{:S(2)}, u32[]{:S(2)}) collective-permute-start(f32[5,3,16,128]{3,2,1,0:T(8,128)S(1)} %get-tuple-element.27), channel_id=1, source_target_pairs={{0,6},{6,12},{12,18},{18,24},{24,30},{30,36},{36,42},{42,48},{48,5... | collective-permute-start | bytes 368648 | tf_op jit(solution)/shard_map/ppermute | solution.py:391
  37.1 0.0 collective-permute-done.3
  37.1 0.7 %collective-permute-start.4 = (f32[5,3,16,128]{3,2,1,0:T(8,128)S(1)}, f32[5,3,16,128]{3,2,1,0:T(8,128)S(1)}, u32[]{:S(2)}, u32[]{:S(2)}) collective-permute-start(f32[5,3,16,128]{3,2,1,0:T(8,128)S(1)} %collective-permute-done.3), channel_id=1, source_target_pairs={{11,762},{377,384},{17,763},{371,385},{23,764},{365,386}} | collective-permute-start | bytes 368648 | tf_op jit(solution)/shard_map/ppermute | solution.py:389
  37.8 0.0 all-to-all-done.got_ref
  37.8 0.6 %relay.1 = f32[64,1,128]{2,1,0:T(1,128)} custom-call(f32[12,16,128]{2,1,0:T(8,128)S(1)} %all-to-all-done.got_ref), custom_call_target="tpu_custom_call" | custom-call | tf_op jit(solution)/shard_map/relay/pallas_call | solution.py:365
  38.4 11.1 %all-to-all-start.1 = ((f32[64,1,128]{2,1,0:T(1,128)}), f32[64,1,128]{2,1,0:T(1,128)S(1)}, u32[]{:S(2)}, u32[]{:S(2)}) async-start(f32[64,1,128]{2,1,0:T(1,128)} %relay.1), calls=%async_computation.1 | async-start | bytes 65536 | tf_op jit(solution)/shard_map/all_to_all | solution.py:366
  49.5 0.4 prepare.1
  50.0 9.0 %all-to-all-done.1.speed_ref = f32[64,1,128]{2,1,0:T(1,128)S(1)} async-done(((f32[64,1,128]{2,1,0:T(1,128)}), f32[64,1,128]{2,1,0:T(1,128)S(1)}, u32[]{:S(2)}, u32[]{:S(2)}) %all-to-all-start.1) | async-done | bytes 32800 | tf_op jit(solution)/shard_map/all_to_all | solution.py:366
  59.0 0.1 peak.1.speed_ref
  59.1 0.0 collective-permute-done.2.seam_ref
  59.1 0.0 collective-permute-done.1.xhi_ref
  59.1 0.0 collective-permute-done.xlo_ref
  59.1 0.0 collective-permute-done.4.helped_ref
  59.1 4.5 %step.1 = (f32[5,128,128]{2,1,0:T(8,128)}, f32[5,128,128]{2,1,0:T(8,128)}) custom-call(f32[3,8,128]{2,1,0:T(8,128)S(1)} %peak.1.speed_ref, f32[5,128,128]{2,1,0:T(8,128)S(1)} %get-tuple-element.15.state_ref, f32[5,3,16,128]{3,2,1,0:T(8,128)S(1)} %collective-permute-done.xlo_ref, f32[5,3,16,128]{3,2,1,0:T(8,128)S(1)} %collective-permute-done.1.xhi_ref, ...), custom_call_target="tpu_custom_call" | custom-call | tf_op jit(solution)/shard_map/step/pallas_call | solution.py:395
  (1 shorter events, 0.0 us)
Async XLA Ops:
  2.6 34.5 %collective-permute-start.3 = (f32[5,3,16,128]{3,2,1,0:T(8,128)S(1)}, f32[5,3,16,128]{3,2,1,0:T(8,128)S(1)}, u32[]{:S(2)}, u32[]{:S(2)}) collective-permute-start(f32[5,3,16,128]{3,2,1,0:T(8,128)S(1)} %get-tuple-element.16), channel_id=1, source_target_pairs={{0,11},{378,377},{1,17},{379,371},{2,23},{380,365}} | collective-permute-start | bytes 368648 | tf_op jit(solution)/shard_map/ppermute | solution.py:388
  3.3 55.8 %collective-permute-start.2 = (f32[5,3,16,128]{3,2,1,0:T(8,128)S(1)}, f32[5,3,16,128]{3,2,1,0:T(8,128)S(1)}, u32[]{:S(2)}, u32[]{:S(2)}) collective-permute-start(f32[5,3,16,128]{3,2,1,0:T(8,128)S(1)} %get-tuple-element.16), channel_id=1, source_target_pairs={{384,378},{762,0},{385,379},{763,1},{386,380},{764,2},{387,381},{7... | collective-permute-start | bytes 368648 | tf_op jit(solution)/shard_map/ppermute | solution.py:387
  4.0 33.8 %all-to-all-start = ((f32[12,16,128]{2,1,0:T(8,128)}), f32[12,16,128]{2,1,0:T(8,128)S(1)}, u32[]{:S(2)}, u32[]{:S(2)}) async-start(f32[12,16,128]{2,1,0:T(8,128)} %get-tuple-element.14), calls=%async_computation | async-start | bytes 196608 | tf_op jit(solution)/shard_map/all_to_all | solution.py:358
  19.7 39.4 %collective-permute-start.1 = (f32[5,3,16,128]{3,2,1,0:T(8,128)S(1)}, f32[5,3,16,128]{3,2,1,0:T(8,128)S(1)}, u32[]{:S(2)}, u32[]{:S(2)}) collective-permute-start(f32[5,3,16,128]{3,2,1,0:T(8,128)S(1)} %get-tuple-element.26), channel_id=1, source_target_pairs={{6,0},{12,6},{18,12},{24,18},{30,24},{36,30},{42,36},{48,42},{54,4... | collective-permute-start | bytes 368648 | tf_op jit(solution)/shard_map/ppermute | solution.py:390
  35.2 24.0 %collective-permute-start = (f32[5,3,16,128]{3,2,1,0:T(8,128)S(1)}, f32[5,3,16,128]{3,2,1,0:T(8,128)S(1)}, u32[]{:S(2)}, u32[]{:S(2)}) collective-permute-start(f32[5,3,16,128]{3,2,1,0:T(8,128)S(1)} %get-tuple-element.27), channel_id=1, source_target_pairs={{0,6},{6,12},{12,18},{18,24},{24,30},{30,36},{36,42},{42,48},{48,5... | collective-permute-start | bytes 368648 | tf_op jit(solution)/shard_map/ppermute | solution.py:391
  37.1 22.0 %collective-permute-start.4 = (f32[5,3,16,128]{3,2,1,0:T(8,128)S(1)}, f32[5,3,16,128]{3,2,1,0:T(8,128)S(1)}, u32[]{:S(2)}, u32[]{:S(2)}) collective-permute-start(f32[5,3,16,128]{3,2,1,0:T(8,128)S(1)} %collective-permute-done.3), channel_id=1, source_target_pairs={{11,762},{377,384},{17,763},{371,385},{23,764},{365,386}} | collective-permute-start | bytes 368648 | tf_op jit(solution)/shard_map/ppermute | solution.py:389
  38.4 20.5 %all-to-all-start.1 = ((f32[64,1,128]{2,1,0:T(1,128)}), f32[64,1,128]{2,1,0:T(1,128)S(1)}, u32[]{:S(2)}, u32[]{:S(2)}) async-start(f32[64,1,128]{2,1,0:T(1,128)} %relay.1), calls=%async_computation.1 | async-start | bytes 65536 | tf_op jit(solution)/shard_map/all_to_all | solution.py:366
